TPU v7x, 8 devices: a whole 2x2x1 slice. The times are simulated.
8 devices in a mesh: rep: 2 (over z, y), ep: 2 (over x), dp: 2 (over core).
Axes of the slice: x: 2, y: 2, z: 1, core: 2. Of those that a mesh axis runs over, the one named last changes fastest.
Arguments:
- tok_in: bfloat16 [32768, 256], P(('rep', 'ep', 'dp'))
- tok_grad: bfloat16 [32768, 256], P(('rep', 'ep', 'dp'))
- route_ids: int32 [2, 32768, 2], P(None, ('rep', 'ep', 'dp'))
- gate_vals: float32 [2, 32768, 2], P(None, ('rep', 'ep', 'dp'))
- w_dense: bfloat16 [2, 256, 256], replicated
- w_gate: bfloat16 [2, 8, 256, 896], P(None, 'ep')
- w_up: bfloat16 [2, 8, 256, 896], P(None, 'ep')
- w_down: bfloat16 [2, 8, 896, 256], P(None, 'ep')
Outputs:
- output 1: bfloat16 [32768, 256], P(('rep', 'ep', 'dp'))
- output 2: bfloat16 [32768, 256], P(('rep', 'ep', 'dp'))
- output 3: bfloat16 [2, 256, 256], replicated
- output 4: bfloat16 [2, 8, 256, 896], P(None, 'ep')
- output 5: bfloat16 [2, 8, 256, 896], P(None, 'ep')
- output 6: bfloat16 [2, 8, 896, 256], P(None, 'ep')
All inputs are finite; a program needn't handle non-finite values.
Results may differ from a plain program's by a relative error of at most 0.02.
Values are sent between devices in bfloat16 or wider.
A program may use at most 1 GiB of HBM per device.

v0:
```python
import jax
import jax.numpy as jnp
from jax import lax
from jax.sharding import PartitionSpec as P

TOK_AXES = ("rep", "ep", "dp")


def slot_tables(route_loc, experts):
    tokens, top_k = route_loc.shape
    capacity = 2 * tokens * top_k // experts
    flat_ids = route_loc.reshape(tokens * top_k)
    expert_hits = (flat_ids[:, None] == jnp.arange(experts, dtype=jnp.int32)[None, :]).astype(jnp.int32)
    slot_rank = jnp.sum((jnp.cumsum(expert_hits, axis=0) - 1) * expert_hits, axis=1)
    slot_of = flat_ids * capacity + slot_rank
    copy_of = jnp.full((experts * capacity,), tokens * top_k, jnp.int32)
    copy_of = copy_of.at[slot_of].set(jnp.arange(tokens * top_k, dtype=jnp.int32))
    return slot_of, copy_of


def layer_forward(tok_loc, route_loc, gate_loc, dense_w, gate_w, up_w, down_w, ep_size):
    tokens, top_k = route_loc.shape
    model_width = tok_loc.shape[1]
    experts = gate_w.shape[0] * ep_size
    capacity = 2 * tokens * top_k // experts
    mixed_val = (tok_loc.astype(jnp.float32) + jnp.dot(tok_loc, dense_w, preferred_element_type=jnp.float32)).astype(jnp.bfloat16)
    slot_of, copy_of = slot_tables(route_loc, experts)
    padded = jnp.concatenate([mixed_val, jnp.zeros((1, model_width), jnp.bfloat16)], axis=0)
    send_buf = jnp.take(padded, copy_of // top_k, axis=0).reshape(experts, capacity, model_width)
    expert_in = lax.all_to_all(send_buf, "ep", 0, 1, tiled=True)
    act_gate = jnp.einsum("end,edf->enf", expert_in, gate_w, preferred_element_type=jnp.float32).astype(jnp.bfloat16)
    act_up = jnp.einsum("end,edf->enf", expert_in, up_w, preferred_element_type=jnp.float32).astype(jnp.bfloat16)
    hidden = (jax.nn.silu(act_gate.astype(jnp.float32)) * act_up.astype(jnp.float32)).astype(jnp.bfloat16)
    expert_out = jnp.einsum("enf,efd->end", hidden, down_w, preferred_element_type=jnp.float32).astype(jnp.bfloat16)
    returned = lax.all_to_all(expert_out, "ep", 1, 0, tiled=True).reshape(experts * capacity, model_width)
    per_copy = jnp.take(returned, slot_of, axis=0).reshape(tokens, top_k, model_width)
    mix_sum = jnp.sum(gate_loc[:, :, None] * per_copy, axis=1)
    tok_out = (mixed_val.astype(jnp.float32) + mix_sum).astype(jnp.bfloat16)
    return tok_out, (tok_loc, slot_of, copy_of, expert_in, act_gate, act_up, hidden)


def layer_backward(grad_out, gate_loc, dense_w, gate_w, up_w, down_w, layer_saved, ep_size):
    tok_loc, slot_of, copy_of, expert_in, act_gate, act_up, hidden = layer_saved
    tokens, top_k = gate_loc.shape
    model_width = grad_out.shape[1]
    experts = gate_w.shape[0] * ep_size
    capacity = copy_of.shape[0] // experts
    gate_pad = jnp.concatenate([gate_loc.reshape(tokens * top_k), jnp.zeros((1,), jnp.float32)])
    grad_pad = jnp.concatenate([grad_out, jnp.zeros((1, model_width), jnp.bfloat16)], axis=0)
    slot_gate = jnp.take(gate_pad, copy_of)
    send_grad = (slot_gate[:, None] * jnp.take(grad_pad, copy_of // top_k, axis=0)).astype(jnp.bfloat16).reshape(experts, capacity, model_width)
    grad_exp_out = lax.all_to_all(send_grad, "ep", 0, 1, tiled=True)
    grad_hidden = jnp.einsum("end,efd->enf", grad_exp_out, down_w, preferred_element_type=jnp.float32)
    grad_down = jnp.einsum("enf,end->efd", hidden, grad_exp_out, preferred_element_type=jnp.float32)
    gate_f = act_gate.astype(jnp.float32)
    sig_gate = jax.nn.sigmoid(gate_f)
    grad_up_act = (grad_hidden * gate_f * sig_gate).astype(jnp.bfloat16)
    grad_gate_act = (grad_hidden * act_up.astype(jnp.float32) * sig_gate * (1.0 + gate_f * (1.0 - sig_gate))).astype(jnp.bfloat16)
    grad_gate = jnp.einsum("end,enf->edf", expert_in, grad_gate_act, preferred_element_type=jnp.float32)
    grad_up = jnp.einsum("end,enf->edf", expert_in, grad_up_act, preferred_element_type=jnp.float32)
    grad_exp_in = (jnp.einsum("enf,edf->end", grad_gate_act, gate_w, preferred_element_type=jnp.float32) + jnp.einsum("enf,edf->end", grad_up_act, up_w, preferred_element_type=jnp.float32)).astype(jnp.bfloat16)
    grad_back = lax.all_to_all(grad_exp_in, "ep", 1, 0, tiled=True).reshape(experts * capacity, model_width)
    grad_mixed = grad_out.astype(jnp.float32) + jnp.sum(jnp.take(grad_back, slot_of, axis=0).reshape(tokens, top_k, model_width), axis=1, dtype=jnp.float32)
    grad_mixed_bf = grad_mixed.astype(jnp.bfloat16)
    grad_dense = lax.dot_general(tok_loc, grad_mixed_bf, (((0,), (0,)), ((), ())), preferred_element_type=jnp.float32)
    grad_tok = (grad_mixed + lax.dot_general(grad_mixed_bf, dense_w, (((1,), (1,)), ((), ())), preferred_element_type=jnp.float32)).astype(jnp.bfloat16)
    return grad_tok, grad_dense, grad_gate, grad_up, grad_down


def solution(mesh):
    ep_size = mesh.shape["ep"]
    tok_spec = P(TOK_AXES, None)
    route_spec = P(None, TOK_AXES, None)
    expert_spec = P(None, "ep", None, None)
    whole_spec = P(None, None, None)

    def device_step(tok_in, tok_grad, route_ids, gate_vals, w_dense, w_gate, w_up, w_down):
        layers = w_dense.shape[0]
        current = tok_in
        saved_all = []
        for layer_idx in range(layers):
            current, layer_saved = layer_forward(current, route_ids[layer_idx], gate_vals[layer_idx], w_dense[layer_idx], w_gate[layer_idx], w_up[layer_idx], w_down[layer_idx], ep_size)
            saved_all.append(layer_saved)
        grad_cur = tok_grad
        dense_sums = []
        gate_sums = []
        up_sums = []
        down_sums = []
        for layer_idx in reversed(range(layers)):
            grad_cur, grad_dense, grad_gate, grad_up, grad_down = layer_backward(grad_cur, gate_vals[layer_idx], w_dense[layer_idx], w_gate[layer_idx], w_up[layer_idx], w_down[layer_idx], saved_all[layer_idx], ep_size)
            dense_sums.insert(0, lax.psum(grad_dense.astype(jnp.bfloat16), TOK_AXES))
            gate_sums.insert(0, lax.psum(lax.psum(grad_gate.astype(jnp.bfloat16), "rep"), "dp"))
            up_sums.insert(0, lax.psum(lax.psum(grad_up.astype(jnp.bfloat16), "rep"), "dp"))
            down_sums.insert(0, lax.psum(lax.psum(grad_down.astype(jnp.bfloat16), "rep"), "dp"))
        return current, grad_cur, jnp.stack(dense_sums), jnp.stack(gate_sums), jnp.stack(up_sums), jnp.stack(down_sums)

    return jax.shard_map(device_step, mesh=mesh, in_specs=(tok_spec, tok_spec, route_spec, route_spec, whole_spec, expert_spec, expert_spec, expert_spec), out_specs=(tok_spec, tok_spec, whole_spec, expert_spec, expert_spec, expert_spec), check_vma=False)
```

profile of v0, /device:TPU:0, one launch (start us, length us, event | category | flops | bytes accessed | tf_op | source)
XLA Modules:
  0.0 1921.8 jit_solution(17101056071811383424)
XLA Ops:
  16.6 30.5 %scatter_custom_fusion = s32[16384]{0:T(1024)S(1)} fusion(s32[8192]{0:T(1024)S(1)} %bitcast.198, s32[8192]{0:T(1024)S(1)} %iota.19, s32[]{:T(128)} %constant.74.clone.1), kind=kCustom, calls=%fused_computation.178 | custom fusion | bytes 65540 | tf_op jit(solution)/shard_map/scatter | solution.py:17
  52.3 64.9 %gather_fusion = bf16[16384,256]{1,0:T(8,128)(2,1)} fusion(bf16[4097,256]{1,0:T(8,128)(2,1)S(1)} %concatenate.18, s32[16384]{0:T(1024)S(1)} %get-tuple-element.47), kind=kCustom, calls=%fused_computation.clone | custom fusion | bytes 16842752 | tf_op jit(solution)/shard_map/jit(_take)/gather | solution.py:29
  117.2 8.0 broadcast_select_fusion.1
  125.3 7.4 all-to-all-start
  149.9 31.0 %scatter_custom_fusion.1 = s32[16384]{0:T(1024)S(1)} fusion(s32[8192]{0:T(1024)S(1)} %bitcast.197, s32[8192]{0:T(1024)S(1)} %iota.20, s32[]{:T(128)} %constant.74.clone.1), kind=kCustom, calls=%fused_computation.176 | custom fusion | bytes 65540 | tf_op jit(solution)/shard_map/scatter | solution.py:17
  181.6 90.5 %gather_fusion.4 = f32[16384]{0:T(1024)S(1)} fusion(f32[8193]{0:T(1024)S(1)} %get-tuple-element.63, s32[16384]{0:T(1024)S(1)} %get-tuple-element.52), kind=kCustom, calls=%fused_computation.2.clone | custom fusion | bytes 196608 | tf_op jit(solution)/shard_map/jit(_take)/gather | solution.py:50
  272.2 64.9 %gather_fusion.5 = bf16[16384,256]{1,0:T(8,128)(2,1)} fusion(bf16[4097,256]{1,0:T(8,128)(2,1)S(1)} %concatenate.21, s32[16384]{0:T(1024)S(1)} %get-tuple-element.53), kind=kCustom, calls=%fused_computation.4.clone | custom fusion | bytes 16842752 | tf_op jit(solution)/shard_map/jit(_take)/gather | solution.py:51
  337.2 7.3 copy.58
  344.5 15.9 convolution_convert_fusion.3
  360.4 36.8 %fusion = (bf16[4,4096,896]{2,1,0:T(8,128)(2,1)}, bf16[4,4096,896]{2,1,0:T(8,128)(2,1)}) fusion(bf16[4,4096,896]{2,1,0:T(8,128)(2,1)} %convolution_convert_fusion.3, bf16[4,4096,256]{2,1,0:T(8,128)(2,1)} %bitcast.178, bf16[2,4,256,896]{3,2,1,0:T(8,128)(2,1)} %param.20), kind=kOutput, calls=%fused_computation.24 | convolution fusion | flops 7648313344 | bytes 98304000 | tf_op jit(solution)/shard_map/end,edf->enf/dot_general | solution.py:32
  397.2 16.9 convolution_convert_fusion.5
  414.1 12.1 copy.59
  433.3 7.6 multiply_convert_fusion.1
  440.9 86.2 %all-to-all-done.1 = bf16[4,4096,256]{2,0,1:T(4,128)(2,1)} async-done(((bf16[4,4096,256]{2,0,1:T(4,128)(2,1)}), bf16[4,4096,256]{2,0,1:T(4,128)(2,1)}, u32[]{:S(2)}, u32[]{:S(2)}) %all-to-all-start.1) | async-done | bytes 8388640 | tf_op jit(solution)/shard_map/all_to_all | solution.py:35
  534.1 7.7 copy.60
  541.8 35.6 %gather_fusion.1 = bf16[8192,256]{1,0:T(8,128)(2,1)} fusion(bf16[16384,256]{1,0:T(8,128)(2,1)} %bitcast.172, s32[8192]{0:T(1024)S(1)} %broadcast_clamp_fusion.3), kind=kCustom, calls=%fused_computation.1.clone | custom fusion | bytes 8421376 | tf_op jit(solution)/shard_map/jit(_take)/gather | solution.py:36
  577.4 8.3 select_convert_fusion.3
  585.8 10.7 reshape.175
  596.5 23.7 %multiply_reduce_fusion.1 = f32[4096,256]{1,0:T(8,128)S(1)} fusion(f32[4096,2,256]{2,1,0:T(2,128)} %reshape.175, f32[4096,2]{1,0:T(8,128)S(1)} %copy-done.13), kind=kLoop, calls=%fused_computation.53 | loop fusion | flops 3145728 | bytes 12615680 | tf_op jit(solution)/shard_map/reduce_sum | solution.py:37
  624.7 64.9 %gather_fusion.2 = bf16[16384,256]{1,0:T(8,128)(2,1)} fusion(bf16[4097,256]{1,0:T(8,128)(2,1)S(1)} %concatenate.19, s32[16384]{0:T(1024)S(1)} %copy-done.28), kind=kCustom, calls=%fused_computation.3.clone | custom fusion | bytes 16842752 | tf_op jit(solution)/shard_map/jit(_take)/gather | solution.py:29
  689.6 8.0 broadcast_select_fusion
  704.8 90.9 %gather_fusion.7 = f32[16384]{0:T(1024)S(1)} fusion(f32[8193]{0:T(1024)S(1)} %copy-done, s32[16384]{0:T(1024)S(1)} %copy-done.39), kind=kCustom, calls=%fused_computation.9.clone | custom fusion | bytes 196608 | tf_op jit(solution)/shard_map/jit(_take)/gather | solution.py:50
  797.0 7.3 copy.69
  804.3 7.3 copy.65
  811.6 16.0 convolution_convert_fusion
  827.6 15.9 convolution_convert_fusion.1
  843.5 61.9 %fusion.19 = (bf16[4,4096,896]{2,1,0:T(8,128)(2,1)}, bf16[4,4096,896]{2,1,0:T(8,128)(2,1)}, bf16[4,4096,896]{2,1,0:T(8,128)(2,1)}) fusion(bf16[4,4096,896]{2,1,0:T(8,128)(2,1)} %convolution_convert_fusion.1, bf16[4,4096,896]{2,1,0:T(8,128)(2,1)} %convolution_convert_fusion, bf16[4,4096,256]{2,1,0:T(8,128)(2,1)} %bitcast.185, bf16[2,4,896,256]{3,2,1,0:T(8,128)(2,1)} %param.21), kind=kOutput, calls=%fused_computation.43 | convolution fusion | flops 7780433920 | bytes 157024256 | tf_op jit(solution)/shard_map/end,efd->enf/dot_general | solution.py:53
  905.5 18.1 fusion.37
  923.5 21.6 %add_convert_fusion.1 = bf16[4,4096,256]{2,1,0:T(8,128)(2,1)} fusion(f32[4,4096,256]{2,1,0:T(8,128)} %fusion.37, bf16[4,4096,896]{2,1,0:T(8,128)(2,1)} %get-tuple-element.43, bf16[2,4,256,896]{3,2,1,0:T(8,128)(2,1)} %param.20), kind=kOutput, calls=%fused_computation.50 | convolution fusion | flops 7524581376 | bytes 56360960 | tf_op jit(solution)/shard_map/enf,edf->end/dot_general | solution.py:61
  945.2 12.2 copy.70
  964.5 17.0 convolution_convert_fusion.4
  981.6 12.2 copy.66
  993.8 18.0 convolution_convert_fusion.6
  1011.8 44.6 %all-to-all-done.5 = bf16[4,4096,256]{2,0,1:T(4,128)(2,1)} async-done(((bf16[4,4096,256]{2,0,1:T(4,128)(2,1)}), bf16[4,4096,256]{2,0,1:T(4,128)(2,1)}, u32[]{:S(2)}, u32[]{:S(2)}) %all-to-all-start.5) | async-done | bytes 8388640 | tf_op jit(solution)/shard_map/all_to_all | solution.py:62
  1063.4 21.2 %convolution_convert_fusion.8 = bf16[4,256,896]{2,1,0:T(8,128)(2,1)} fusion(bf16[4,4096,256]{2,1,0:T(8,128)(2,1)} %bitcast.175, bf16[4,4096,896]{2,1,0:T(8,128)(2,1)} %get-tuple-element.43), kind=kOutput, calls=%fused_computation.99 | convolution fusion | flops 7517110272 | bytes 39583744 | tf_op jit(solution)/shard_map/end,enf->edf/dot_general | solution.py:60
  1084.6 7.8 copy.71
  1092.4 62.1 %all-to-all-done.3 = bf16[4,4096,256]{2,0,1:T(4,128)(2,1)} async-done(((bf16[4,4096,256]{2,0,1:T(4,128)(2,1)}), bf16[4,4096,256]{2,0,1:T(4,128)(2,1)}, u32[]{:S(2)}, u32[]{:S(2)}) %all-to-all-start.3) | async-done | bytes 8388640 | tf_op jit(solution)/shard_map/all_to_all | solution.py:35
  1154.5 7.8 copy.67
  1162.3 35.4 %gather_fusion.6 = bf16[8192,256]{1,0:T(8,128)(2,1)} fusion(bf16[16384,256]{1,0:T(8,128)(2,1)} %bitcast.169, s32[8192]{0:T(1024)S(1)} %copy-done.37), kind=kCustom, calls=%fused_computation.7.clone | custom fusion | bytes 8421376 | tf_op jit(solution)/shard_map/jit(_take)/gather | solution.py:63
  1197.7 35.4 %gather_fusion.3 = bf16[8192,256]{1,0:T(8,128)(2,1)} fusion(bf16[16384,256]{1,0:T(8,128)(2,1)} %bitcast.170, s32[8192]{0:T(1024)S(1)} %copy-done.37), kind=kCustom, calls=%fused_computation.6.clone | custom fusion | bytes 8421376 | tf_op jit(solution)/shard_map/jit(_take)/gather | solution.py:36
  1233.1 10.7 select_convert_fusion.1
  1243.9 10.8 reshape.177
  1254.7 25.1 %reduce_sum.64 = f32[4096,256]{1,0:T(8,128)} reduce(f32[4096,2,256]{2,1,0:T(2,128)} %reshape.177, f32[]{:T(128)} %constant.81.clone.1), dimensions={1}, to_apply=%region_10.14 | reduce | flops 1048576 | bytes 12582916 | tf_op jit(solution)/shard_map/reduce_sum | solution.py:63
  1285.7 64.9 %gather_fusion.8 = bf16[16384,256]{1,0:T(8,128)(2,1)} fusion(bf16[4097,256]{1,0:T(8,128)(2,1)S(1)} %concatenate.23, s32[16384]{0:T(1024)S(1)} %copy-done.26), kind=kCustom, calls=%fused_computation.5.clone | custom fusion | bytes 16842752 | tf_op jit(solution)/shard_map/jit(_take)/gather | solution.py:51
  1350.7 7.6 multiply_convert_fusion
  1365.3 20.8 %convolution_convert_fusion.10 = bf16[4,256,896]{2,1,0:T(8,128)(2,1)} fusion(bf16[4,4096,256]{2,1,0:T(8,128)(2,1)} %bitcast.176, bf16[4,4096,896]{2,1,0:T(8,128)(2,1)} %get-tuple-element.44), kind=kOutput, calls=%fused_computation.101 | convolution fusion | flops 7517110272 | bytes 39583744 | tf_op jit(solution)/shard_map/end,enf->edf/dot_general | solution.py:59
  1386.0 69.5 %all-to-all-done.6 = bf16[8,2048,256]{2,1,0:T(8,128)(2,1)} async-done(((bf16[8,2048,256]{2,1,0:T(8,128)(2,1)}), bf16[8,2048,256]{2,1,0:T(8,128)(2,1)}, u32[]{:S(2)}, u32[]{:S(2)}) %all-to-all-start.6) | async-done | bytes 8388640 | tf_op jit(solution)/shard_map/all_to_all | solution.py:52
  1462.7 18.1 convolution_convert_fusion.7
  1480.8 51.4 %fusion.13 = (bf16[4,4096,896]{2,1,0:T(8,128)(2,1)}, bf16[4,4096,896]{2,1,0:T(8,128)(2,1)}) fusion(bf16[4,4096,896]{2,1,0:T(8,128)(2,1)} %convolution_convert_fusion.3, bf16[4,4096,896]{2,1,0:T(8,128)(2,1)} %get-tuple-element.61, bf16[4,4096,256]{2,1,0:T(8,128)(2,1)} %bitcast.188, bf16[2,4,896,256]{3,2,1,0:T(8,128)(2,1)} %param.21), kind=kOutput, calls=%fused_computation.37 | convolution fusion | flops 7736393728 | bytes 127664128 | tf_op jit(solution)/shard_map/end,efd->enf/dot_general | solution.py:53
  1532.2 20.7 %convolution_convert_fusion.9 = bf16[4,256,896]{2,1,0:T(8,128)(2,1)} fusion(bf16[4,4096,256]{2,1,0:T(8,128)(2,1)} %bitcast.179, bf16[4,4096,896]{2,1,0:T(8,128)(2,1)} %get-tuple-element.41), kind=kOutput, calls=%fused_computation.100 | convolution fusion | flops 7517110272 | bytes 39583744 | tf_op jit(solution)/shard_map/end,enf->edf/dot_general | solution.py:60
  1553.0 21.1 %convolution_convert_fusion.11 = bf16[4,256,896]{2,1,0:T(8,128)(2,1)} fusion(bf16[4,4096,256]{2,1,0:T(8,128)(2,1)} %bitcast.180, bf16[4,4096,896]{2,1,0:T(8,128)(2,1)} %get-tuple-element.42), kind=kOutput, calls=%fused_computation.102 | convolution fusion | flops 7517110272 | bytes 39583744 | tf_op jit(solution)/shard_map/end,enf->edf/dot_general | solution.py:59
  1574.1 18.1 fusion.45
  1592.1 21.6 %add_convert_fusion = bf16[4,4096,256]{2,1,0:T(8,128)(2,1)} fusion(f32[4,4096,256]{2,1,0:T(8,128)} %fusion.45, bf16[4,4096,896]{2,1,0:T(8,128)(2,1)} %get-tuple-element.41, bf16[2,4,256,896]{3,2,1,0:T(8,128)(2,1)} %param.20), kind=kOutput, calls=%fused_computation.48 | convolution fusion | flops 7524581376 | bytes 56360960 | tf_op jit(solution)/shard_map/enf,edf->end/dot_general | solution.py:61
  1613.7 12.3 copy.74
  1639.1 83.7 %all-to-all-done.7 = bf16[4,4096,256]{2,0,1:T(4,128)(2,1)} async-done(((bf16[4,4096,256]{2,0,1:T(4,128)(2,1)}), bf16[4,4096,256]{2,0,1:T(4,128)(2,1)}, u32[]{:S(2)}, u32[]{:S(2)}) %all-to-all-start.7) | async-done | bytes 8388640 | tf_op jit(solution)/shard_map/all_to_all | solution.py:62
  1722.7 7.7 copy.75
  1730.5 35.4 %gather_fusion.9 = bf16[8192,256]{1,0:T(8,128)(2,1)} fusion(bf16[16384,256]{1,0:T(8,128)(2,1)} %bitcast.171, s32[8192]{0:T(1024)S(1)} %copy-done.36), kind=kCustom, calls=%fused_computation.8.clone | custom fusion | bytes 8421376 | tf_op jit(solution)/shard_map/jit(_take)/gather | solution.py:63
  1765.9 8.4 select_convert_fusion
  1774.3 10.6 reshape.178
  1784.8 25.0 %reduce_sum.65 = f32[4096,256]{1,0:T(8,128)} reduce(f32[4096,2,256]{2,1,0:T(2,128)} %reshape.178, f32[]{:T(128)} %constant.81.clone.1), dimensions={1}, to_apply=%region_11.15 | reduce | flops 1048576 | bytes 12582916 | tf_op jit(solution)/shard_map/reduce_sum | solution.py:63
  1814.3 8.1 all-reduce.15.cloned.1.call-done
  1824.4 10.8 reshape.176
  1835.2 23.8 %multiply_reduce_fusion = f32[4096,256]{1,0:T(8,128)S(1)} fusion(f32[4096,2,256]{2,1,0:T(2,128)} %reshape.176, f32[4096,2]{1,0:T(8,128)} %copy.61), kind=kLoop, calls=%fused_computation.52 | loop fusion | flops 3145728 | bytes 12615680 | tf_op jit(solution)/shard_map/reduce_sum | solution.py:37
  1870.5 35.7 %all-reduce.13.cloned.1.call-done = (bf16[1,4,256,896]{3,2,1,0:T(8,128)(2,1)}, bf16[1,4,256,896]{3,2,1,0:T(8,128)(2,1)}, bf16[1,4,256,896]{3,2,1,0:T(8,128)(2,1)...) async-done(((bf16[1,4,256,896]{3,2,1,0:T(8,128)(2,1)}, bf16[1,4,256,896]{3,2,1,0:T(8,128)(2,1)}, ...) | async-done | bytes 11010064 | tf_op jit(solution)/shard_map/psum | solution.py:92
  (171 shorter events, 133.3 us)
Async XLA Ops:
  7.2 40.8 %copy-start.19 = (bf16[2,256,256]{2,1,0:T(8,128)(2,1)S(1)}, bf16[2,256,256]{2,1,0:T(8,128)(2,1)}, u32[]{:S(2)}) copy-start(bf16[2,256,256]{2,1,0:T(8,128)(2,1)} %param.18) | copy-start | bytes 786436
  47.1 0.8 copy-start.23
  47.2 70.0 %copy-start.40 = (pred[16384]{0:T(1024)(128)(4,1)}, pred[16384]{0:T(1024)(128)(4,1)S(1)}, u32[]{:S(2)}) copy-start(pred[16384]{0:T(1024)(128)(4,1)S(1)} %compare_and_fusion.1) | copy-start | bytes 49156
  47.9 69.3 %copy-start.25 = (s32[16384]{0:T(1024)}, s32[16384]{0:T(1024)S(1)}, u32[]{:S(2)}) copy-start(s32[16384]{0:T(1024)S(1)} %get-tuple-element.47) | copy-start | bytes 196612
  50.9 1.3 copy-start.3
  125.2 7.4 copy-start.45
  125.3 211.9 %all-to-all-start = ((bf16[8,2048,256]{2,1,0:T(8,128)(2,1)}), bf16[8,2048,256]{2,1,0:T(8,128)(2,1)}, u32[]{:S(2)}, u32[]{:S(2)}) async-start(bf16[8,2048,256]{2,1,0:T(8,128)(2,1)} %bitcast.181), calls=%async_computation | async-start | bytes 16777216 | tf_op jit(solution)/shard_map/all_to_all | solution.py:30
  136.4 12.6 copy-start.29
  149.3 0.6 copy-start.32
  181.6 90.6 %copy-start.27 = (s32[16384]{0:T(1024)}, s32[16384]{0:T(1024)S(1)}, u32[]{:S(2)}) copy-start(s32[16384]{0:T(1024)S(1)} %get-tuple-element.53) | copy-start | bytes 196612
  337.1 204.7 %copy-start.35 = (s32[8192]{0:T(1024)}, s32[8192]{0:T(1024)S(1)}, u32[]{:S(2)}) copy-start(s32[8192]{0:T(1024)S(1)} %broadcast_clamp_fusion.3) | copy-start | bytes 98308
  337.2 7.3 copy-start.11
  426.2 100.9 %all-to-all-start.1 = ((bf16[4,4096,256]{2,0,1:T(4,128)(2,1)}), bf16[4,4096,256]{2,0,1:T(4,128)(2,1)}, u32[]{:S(2)}, u32[]{:S(2)}) async-start(bf16[4,4096,256]{2,0,1:T(4,128)(2,1)} %copy.59), calls=%async_computation.1 | async-start | bytes 16777216 | tf_op jit(solution)/shard_map/all_to_all | solution.py:35
  433.2 144.2 %copy-start.43 = (pred[8192]{0:T(1024)(128)(4,1)}, pred[8192]{0:T(1024)(128)(4,1)S(1)}, u32[]{:S(2)}) copy-start(pred[8192]{0:T(1024)(128)(4,1)S(1)} %compare_and_fusion.3) | copy-start | bytes 24580
  527.1 170.5 %all-to-all-start.4 = ((bf16[8,2048,256]{2,1,0:T(8,128)(2,1)}), bf16[8,2048,256]{2,1,0:T(8,128)(2,1)}, u32[]{:S(2)}, u32[]{:S(2)}) async-start(bf16[8,2048,256]{2,1,0:T(8,128)(2,1)} %bitcast.182), calls=%async_computation.4 | async-start | bytes 16777216 | tf_op jit(solution)/shard_map/all_to_all | solution.py:52
  585.8 10.7 copy-start.13
  596.5 25.7 %copy-start.4 = (bf16[4096,256]{1,0:T(8,128)(2,1)S(1)}, bf16[4096,256]{1,0:T(8,128)(2,1)}, u32[]{:S(2)}) copy-start(bf16[4096,256]{1,0:T(8,128)(2,1)} %copy-done.3) | copy-start | bytes 6291460
  596.5 25.7 %copy-start.20 = (bf16[2,256,256]{2,1,0:T(8,128)(2,1)S(1)}, bf16[2,256,256]{2,1,0:T(8,128)(2,1)}, u32[]{:S(2)}) copy-start(bf16[2,256,256]{2,1,0:T(8,128)(2,1)} %param.18) | copy-start | bytes 786436
  620.2 1.9 copy-start.1
  622.2 2.5 copy-start.28
  623.2 1.3 copy-start.9
  697.6 7.1 copy-start
  697.6 7.1 copy-start.39
  697.6 106.7 %all-to-all-start.2 = ((bf16[8,2048,256]{2,1,0:T(8,128)(2,1)}), bf16[8,2048,256]{2,1,0:T(8,128)(2,1)}, u32[]{:S(2)}, u32[]{:S(2)}) async-start(bf16[8,2048,256]{2,1,0:T(8,128)(2,1)} %bitcast.183), calls=%async_computation.2 | async-start | bytes 16777216 | tf_op jit(solution)/shard_map/all_to_all | solution.py:30
  704.7 91.0 %copy-start.30 = (s32[8192]{0:T(1024)S(1)}, s32[8192]{0:T(1024)}, u32[]{:S(2)}) copy-start(s32[8192]{0:T(1024)} %copy-done.29) | copy-start | bytes 98308
  704.7 91.0 %copy-start.33 = (s32[8192]{0:T(1024)S(1)}, s32[8192]{0:T(1024)}, u32[]{:S(2)}) copy-start(s32[8192]{0:T(1024)} %copy-done.32) | copy-start | bytes 98308
  704.7 91.6 %copy-start.24 = (s32[16384]{0:T(1024)S(1)}, s32[16384]{0:T(1024)}, u32[]{:S(2)}) copy-start(s32[16384]{0:T(1024)} %copy-done.23) | copy-start | bytes 196612
  804.3 7.3 copy-start.14
  811.6 16.0 copy-start.12
  957.4 7.1 copy-start.31
  957.4 7.1 copy-start.34
  957.4 99.0 %all-to-all-start.5 = ((bf16[4,4096,256]{2,0,1:T(4,128)(2,1)}), bf16[4,4096,256]{2,0,1:T(4,128)(2,1)}, u32[]{:S(2)}, u32[]{:S(2)}) async-start(bf16[4,4096,256]{2,0,1:T(4,128)(2,1)} %copy.70), calls=%async_computation.5 | async-start | bytes 16777216 | tf_op jit(solution)/shard_map/all_to_all | solution.py:62
  1056.4 98.1 %all-to-all-start.3 = ((bf16[4,4096,256]{2,0,1:T(4,128)(2,1)}), bf16[4,4096,256]{2,0,1:T(4,128)(2,1)}, u32[]{:S(2)}, u32[]{:S(2)}) async-start(bf16[4,4096,256]{2,0,1:T(4,128)(2,1)} %copy.66), calls=%async_computation.3 | async-start | bytes 16777216 | tf_op jit(solution)/shard_map/all_to_all | solution.py:35
  1154.5 7.8 copy-start.37
  1254.7 25.1 %copy-start.8 = (bf16[4096,256]{1,0:T(8,128)(2,1)S(1)}, bf16[4096,256]{1,0:T(8,128)(2,1)}, u32[]{:S(2)}) copy-start(bf16[4096,256]{1,0:T(8,128)(2,1)} %param.15) | copy-start | bytes 6291460
  1254.7 25.1 %copy-start.21 = (bf16[2,256,256]{2,1,0:T(8,128)(2,1)S(1)}, bf16[2,256,256]{2,1,0:T(8,128)(2,1)}, u32[]{:S(2)}) copy-start(bf16[2,256,256]{2,1,0:T(8,128)(2,1)} %param.18) | copy-start | bytes 786436
  1279.8 5.9 copy-start.26
  1284.2 1.3 copy-start.6
  1285.7 64.9 %copy-start.38 = (f32[16384]{0:T(1024)S(1)}, f32[16384]{0:T(1024)}, u32[]{:S(2)}) copy-start(f32[16384]{0:T(1024)} %and_select_fusion) | copy-start | bytes 196612
  1285.7 64.9 %copy-start.41 = (pred[16384]{0:T(1024)(128)(4,1)S(1)}, pred[16384]{0:T(1024)(128)(4,1)}, u32[]{:S(2)}) copy-start(pred[16384]{0:T(1024)(128)(4,1)} %copy-done.40) | copy-start | bytes 49156
  1358.3 97.3 %all-to-all-start.6 = ((bf16[8,2048,256]{2,1,0:T(8,128)(2,1)}), bf16[8,2048,256]{2,1,0:T(8,128)(2,1)}, u32[]{:S(2)}, u32[]{:S(2)}) async-start(bf16[8,2048,256]{2,1,0:T(8,128)(2,1)} %bitcast.184), calls=%async_computation.6 | async-start | bytes 16777216 | tf_op jit(solution)/shard_map/all_to_all | solution.py:52
  1365.2 457.1 %all-reduce.15.cloned.1.call-start = ((), (), s32[]{:S(2)}) async-start(), calls=%async_computation.10 | async-start | bytes 22020096 | tf_op jit(solution)/shard_map/psum | solution.py:92
  1626.0 7.2 copy-start.5
  1626.0 96.7 %all-to-all-start.7 = ((bf16[4,4096,256]{2,0,1:T(4,128)(2,1)}), bf16[4,4096,256]{2,0,1:T(4,128)(2,1)}, u32[]{:S(2)}, u32[]{:S(2)}) async-start(bf16[4,4096,256]{2,0,1:T(4,128)(2,1)} %copy.74), calls=%async_computation.7 | async-start | bytes 16777216 | tf_op jit(solution)/shard_map/all_to_all | solution.py:62
  1633.1 235.6 %all-reduce.11.cloned.1.call-start = ((), (), s32[]{:S(2)}) async-start(), calls=%async_computation.8 | async-start | bytes 524288 | tf_op jit(solution)/shard_map/psum | solution.py:91
  1722.7 7.7 copy-start.36
  1730.5 35.4 %copy-start.44 = (pred[8192]{0:T(1024)(128)(4,1)S(1)}, pred[8192]{0:T(1024)(128)(4,1)}, u32[]{:S(2)}) copy-start(pred[8192]{0:T(1024)(128)(4,1)} %copy-done.43) | copy-start | bytes 24580
  1784.8 25.0 %copy-start.7 = (bf16[4096,256]{1,0:T(8,128)(2,1)S(1)}, bf16[4096,256]{1,0:T(8,128)(2,1)}, u32[]{:S(2)}) copy-start(bf16[4096,256]{1,0:T(8,128)(2,1)} %copy-done.6) | copy-start | bytes 6291460
  1809.9 12.5 copy-start.42
  1814.2 92.0 %all-reduce.13.cloned.1.call-start = ((), (), s32[]{:S(2)}) async-start(), calls=%async_computation.9 | async-start | bytes 22020096 | tf_op jit(solution)/shard_map/psum | solution.py:92
  1835.2 23.8 %copy-start.10 = (bf16[4096,256]{1,0:T(8,128)(2,1)S(1)}, bf16[4096,256]{1,0:T(8,128)(2,1)}, u32[]{:S(2)}) copy-start(bf16[4096,256]{1,0:T(8,128)(2,1)} %copy-done.9) | copy-start | bytes 6291460
  1835.2 25.8 %copy-start.2 = (f32[4096,256]{1,0:T(8,128)S(1)}, f32[4096,256]{1,0:T(8,128)}, u32[]{:S(2)}) copy-start(f32[4096,256]{1,0:T(8,128)} %reduce_sum.65) | copy-start | bytes 12582916
  1835.2 25.8 %copy-start.22 = (bf16[2,256,256]{2,1,0:T(8,128)(2,1)S(1)}, bf16[2,256,256]{2,1,0:T(8,128)(2,1)}, u32[]{:S(2)}) copy-start(bf16[2,256,256]{2,1,0:T(8,128)(2,1)} %param.18) | copy-start | bytes 786436
  1906.2 4.4 copy-start.17
  1906.2 4.4 copy-start.18
  1906.2 6.7 copy-start.15
  1906.3 6.7 copy-start.16
Sparse Core Ops, SparseCore 0:
  1574.2 248.1 all-reduce.14
  1826.0 42.6 all-reduce.10
  1871.8 34.3 all-reduce.12
where the time goes:
time: 1930 us; the launch traced here: 1920 us
  local copies, waits for them, and re-layouts  825 us (43%)
  matrix products  452 us (23%)
  waiting for transfers between devices  395 us (20%)
  other arithmetic  178 us (9%)
  starting transfers between devices  56.8 us (3%)
    gather x2, local copies, waits for them, and re-layouts, layer_backward(): slot_gate = jnp.take(gate_pad, copy_of)  181 us
    all_to_all x2, waiting for transfers between devices, layer_forward(): lax.all_to_all(expert_out, 'ep', 1, 0, tiled=True)  148 us
    gather x2, local copies, waits for them, and re-layouts, layer_backward(): jnp.take(grad_pad, copy_of // top_k, axis=0)  130 us
    gather x2, local copies, waits for them, and re-layouts, layer_forward(): jnp.take(padded, copy_of // top_k, axis=0)  130 us
    all_to_all x2, waiting for transfers between devices, layer_backward(): lax.all_to_all(grad_exp_in, 'ep', 1, 0, tiled=True)  128 us
    dot_general x2, matrix products, layer_backward(): jnp.einsum('end,efd->enf', grad_exp_out, down_w, preferred_element_type=j...  113 us
    gather x2, local copies, waits for them, and re-layouts, layer_forward(): jnp.take(returned, slot_of, axis=0).reshape(tokens, top_k, model_width)  71 us
    gather x2, local copies, waits for them, and re-layouts, layer_backward(): jnp.take(grad_back, slot_of, axis=0).reshape(tokens, top_k, model_width)  70.8 us
  transfers between devices with their start and end apart: 11, of which 8 were waited for; matrix products, arithmetic and copies ran while one was open for 40% of the time, Pallas kernels for 0%

commit v1 on v0

v1 whole, which is shorter than its diff:
```python
import functools

import jax
import jax.numpy as jnp
from jax import lax
from jax.experimental import pallas as pl
from jax.experimental.pallas import tpu as pltpu
from jax.sharding import PartitionSpec as P

TOK_AXES = ("rep", "ep", "dp")
CHUNK = 256
GRAN = 16
TILE = 256
F32 = jnp.float32
BF16 = jnp.bfloat16


def dot_nn(a, b):
    return jnp.dot(a, b, preferred_element_type=F32)


def dot_nt(a, b):
    return lax.dot_general(a, b, (((1,), (1,)), ((), ())), preferred_element_type=F32)


def dot_tn(a, b):
    return lax.dot_general(a, b, (((0,), (0,)), ((), ())), preferred_element_type=F32)


def sizes(tokens, top_k, experts):
    chunks = tokens // CHUNK
    local_rows = -(-(CHUNK * top_k + experts * (GRAN - 1)) // 128) * 128
    max_gran = chunks * ((CHUNK * top_k + experts * (GRAN - 1)) // GRAN)
    max_tiles = (max_gran + experts * (TILE // GRAN - 1)) // (TILE // GRAN)
    return chunks, local_rows, max_tiles


def route_tables(ids, experts):
    layers, top_k, tokens = ids.shape
    chunks, local_rows, max_tiles = sizes(tokens, top_k, experts)
    per_tile = TILE // GRAN
    e_iota = jnp.arange(experts, dtype=jnp.int32)
    onehot = ids[:, :, None, :] == e_iota[None, None, :, None]
    hit = jnp.any(onehot, axis=1).astype(BF16).reshape(layers * experts * chunks, CHUNK)
    before = (jnp.arange(CHUNK)[:, None] < jnp.arange(CHUNK)[None, :]).astype(BF16)
    rank = dot_nn(hit, before).astype(jnp.int32).reshape(layers, experts, chunks, CHUNK)
    count = jnp.sum(hit.astype(F32), axis=1).astype(jnp.int32).reshape(layers, experts, chunks)
    grans = (count + GRAN - 1) // GRAN
    lower_e = (e_iota[:, None] > e_iota[None, :]).astype(jnp.int32)
    k_iota = jnp.arange(chunks, dtype=jnp.int32)
    lower_k = (k_iota[:, None] > k_iota[None, :]).astype(jnp.int32)
    seg_start = jnp.sum(grans[:, None, :, :] * lower_e[None, :, :, None], axis=2)
    exp_grans = jnp.sum(grans, axis=2)
    tiles = (exp_grans + per_tile - 1) // per_tile
    tile_start = jnp.sum(tiles[:, None, :] * lower_e[None], axis=2)
    place = tile_start[:, :, None] * per_tile + jnp.sum(grans[:, :, None, :] * lower_k[None, None], axis=3)
    slot_e = (seg_start[..., None] * GRAN + rank).reshape(layers, 1, experts, tokens)
    slot = jnp.sum(jnp.where(onehot, slot_e, 0), axis=2)
    g_iota = jnp.arange(local_rows // GRAN, dtype=jnp.int32)
    rel = g_iota[None, None, :, None] - seg_start.transpose(0, 2, 1)[:, :, None, :]
    inside = (rel >= 0) & (rel < grans.transpose(0, 2, 1)[:, :, None, :])
    spare = max_tiles * per_tile
    table = spare + jnp.sum(jnp.where(inside, place.transpose(0, 2, 1)[:, :, None, :] + rel - spare, 0), axis=3)
    meta = jnp.stack([tile_start, tiles, tile_start * per_tile + exp_grans], axis=1)
    return slot, table.reshape(layers, -1), meta.reshape(layers, -1)


def layer_kernel(cfg, table, meta, x_ref, dy_ref, slot_r, slot_c, gate_c, wd_ref, w1_ref, w3_ref, w2_ref, *refs):
    fwd, bwd, tokens, experts, ff, local_rows, max_tiles = cfg
    refs = list(refs)
    y_ref = refs.pop(0) if fwd else None
    if bwd:
        gx_ref, gwd_ref, g1_ref, g3_ref, g2_ref = refs[:5]
        refs = refs[5:]
    zo = refs.pop(0)
    hs = refs.pop(0)
    oloc = refs.pop(0) if fwd else None
    if bwd:
        dd, das, dbs, a1, a3, a2, awd, dloc = refs
    chunks = tokens // CHUNK
    grans = local_rows // GRAN
    e = pl.program_id(0)

    def granule(i):
        return pl.ds(pl.multiple_of(i * GRAN, GRAN), GRAN)

    def rows_of(k):
        return pl.ds(pl.multiple_of(k * CHUNK, CHUNK), CHUNK)

    def mixed(x_c):
        return (x_c.astype(F32) + dot_nn(x_c, wd_ref[...])).astype(BF16)

    @pl.when(e == 0)
    def _():
        @pl.loop(0, chunks)
        def _(k):
            rows = rows_of(k)
            u = mixed(x_ref[rows, :])
            r_iota = lax.broadcasted_iota(jnp.int32, (local_rows, CHUNK), 0)
            p0 = (slot_r[0:1, rows] == r_iota)
            p1 = (slot_r[1:2, rows] == r_iota)
            one = jnp.ones((), F32)
            zero = jnp.zeros((), F32)
            both = jnp.where(p0 | p1, one, zero).astype(BF16)
            z = dot_nn(both, u).astype(BF16)
            if bwd:
                dy = dy_ref[rows, :].astype(F32)
                d0 = (gate_c[rows, 0:1] * dy).astype(BF16)
                d1 = (gate_c[rows, 1:2] * dy).astype(BF16)
                p0b = jnp.where(p0, one, zero).astype(BF16)
                p1b = jnp.where(p1, one, zero).astype(BF16)
                d = (dot_nn(p0b, d0) + dot_nn(p1b, d1)).astype(BF16)
            for g in range(grans):
                to = granule(table[k * grans + g])
                zo[to, :] = z[g * GRAN:(g + 1) * GRAN, :]
                if bwd:
                    dd[to, :] = d[g * GRAN:(g + 1) * GRAN, :]

        if bwd:
            awd[...] = jnp.zeros_like(awd)

    first = meta[e]
    tiles = meta[experts + e]
    used = meta[2 * experts + e]

    @pl.loop(used, (first + tiles) * (TILE // GRAN))
    def _(g):
        zo[granule(g), :] = jnp.zeros((GRAN, zo.shape[1]), BF16)
        if bwd:
            dd[granule(g), :] = jnp.zeros((GRAN, zo.shape[1]), BF16)

    if bwd:
        a1[...] = jnp.zeros_like(a1)
        a3[...] = jnp.zeros_like(a3)
        a2[...] = jnp.zeros_like(a2)

    @pl.loop(0, tiles)
    def _(i):
        rows = pl.ds(pl.multiple_of((first + i) * TILE, TILE), TILE)
        z = zo[rows, :]
        for f0 in range(0, ff, 256):
            cols = slice(f0, min(f0 + 256, ff))
            a = dot_nn(z, w1_ref[0, :, cols]).astype(BF16).astype(F32)
            b = dot_nn(z, w3_ref[0, :, cols]).astype(BF16).astype(F32)
            sig = jax.nn.sigmoid(a)
            act = a * sig
            hs[:, cols] = (act * b).astype(BF16)
            if bwd:
                dh = dot_nt(dd[rows, :], w2_ref[0, cols, :])
                dbs[:, cols] = (dh * act).astype(BF16)
                das[:, cols] = (dh * b * (sig * (1.0 + a * (1.0 - sig)))).astype(BF16)
        if bwd:
            d = dd[rows, :]
            a1[...] += dot_tn(z, das[...])
            a3[...] += dot_tn(z, dbs[...])
            a2[...] += dot_tn(d, hs[...])
            dd[rows, :] = (dot_nt(das[...], w1_ref[0]) + dot_nt(dbs[...], w3_ref[0])).astype(BF16)
        if fwd:
            zo[rows, :] = dot_nn(hs[...], w2_ref[0]).astype(BF16)

    if bwd:
        g1_ref[0] = a1[...].astype(BF16)
        g3_ref[0] = a3[...].astype(BF16)
        g2_ref[0] = a2[...].T.astype(BF16)

    @pl.when(e == experts - 1)
    def _():
        @pl.loop(0, chunks)
        def _(k):
            rows = rows_of(k)
            x_c = x_ref[rows, :]
            for g in range(grans):
                frm = granule(table[k * grans + g])
                if fwd:
                    oloc[g * GRAN:(g + 1) * GRAN, :] = zo[frm, :]
                if bwd:
                    dloc[g * GRAN:(g + 1) * GRAN, :] = dd[frm, :]
            c_iota = lax.broadcasted_iota(jnp.int32, (CHUNK, local_rows), 1)
            p0 = slot_c[rows, 0:1] == c_iota
            p1 = slot_c[rows, 1:2] == c_iota
            one = jnp.ones((), F32)
            zero = jnp.zeros((), F32)
            if fwd:
                o0 = dot_nn(jnp.where(p0, one, zero).astype(BF16), oloc[...])
                o1 = dot_nn(jnp.where(p1, one, zero).astype(BF16), oloc[...])
                mix = gate_c[rows, 0:1] * o0 + gate_c[rows, 1:2] * o1
                y_ref[rows, :] = (mixed(x_c).astype(F32) + mix).astype(BF16)
            if bwd:
                both = jnp.where(p0 | p1, one, zero).astype(BF16)
                gm = dy_ref[rows, :].astype(F32) + dot_nn(both, dloc[...])
                gmb = gm.astype(BF16)
                awd[...] += dot_tn(x_c, gmb)
                gx_ref[rows, :] = (gm + dot_nt(gmb, wd_ref[...])).astype(BF16)

        if bwd:
            gwd_ref[...] = awd[...].astype(BF16)


def run_layer(fwd, bwd, x, dy, slot, slot_t, gate, table, meta, wd, w1, w3, w2, name):
    tokens, width = x.shape
    experts, _, ff = w1.shape
    top_k = slot.shape[0]
    chunks, local_rows, max_tiles = sizes(tokens, top_k, experts)
    buf_rows = (max_tiles + 1) * TILE
    cfg = (fwd, bwd, tokens, experts, ff, local_rows, max_tiles)

    def whole(shape):
        return pl.BlockSpec(shape, lambda e, *_: (0,) * len(shape))

    def by_expert(shape):
        return pl.BlockSpec((1,) + shape, lambda e, *_: (e, 0, 0))

    tok = whole((tokens, width))
    in_specs = [tok, tok if bwd else whole((8, width)), whole(slot.shape), whole(slot_t.shape), whole(gate.shape), whole(wd.shape), by_expert((width, ff)), by_expert((width, ff)), by_expert((ff, width))]
    out_shape, out_specs = [], []
    tok_shape = jax.ShapeDtypeStruct((tokens, width), BF16)
    if fwd:
        out_shape.append(tok_shape)
        out_specs.append(tok)
    if bwd:
        out_shape += [tok_shape, jax.ShapeDtypeStruct(wd.shape, BF16)] + [jax.ShapeDtypeStruct(w.shape, BF16) for w in (w1, w3, w2)]
        out_specs += [tok, whole(wd.shape), by_expert((width, ff)), by_expert((width, ff)), by_expert((ff, width))]
    scratch = [pltpu.VMEM((buf_rows, width), BF16), pltpu.VMEM((TILE, ff), BF16)]
    if fwd:
        scratch.append(pltpu.VMEM((local_rows, width), BF16))
    if bwd:
        scratch += [pltpu.VMEM((buf_rows, width), BF16), pltpu.VMEM((TILE, ff), BF16), pltpu.VMEM((TILE, ff), BF16)]
        scratch += [pltpu.VMEM((width, ff), F32)] * 3
        scratch += [pltpu.VMEM((width, width), F32), pltpu.VMEM((local_rows, width), BF16)]
    matmuls = (9 if fwd else 8) if bwd else 3
    copies = tokens * top_k
    return pl.pallas_call(
        functools.partial(layer_kernel, cfg),
        out_shape=out_shape,
        grid_spec=pltpu.PrefetchScalarGridSpec(num_scalar_prefetch=2, grid=(experts,), in_specs=in_specs, out_specs=out_specs, scratch_shapes=scratch),
        compiler_params=pltpu.CompilerParams(dimension_semantics=("arbitrary",), vmem_limit_bytes=60 * 1024 * 1024),
        cost_estimate=pl.CostEstimate(flops=2 * matmuls * copies * width * ff, bytes_accessed=3 * experts * width * ff * 2, transcendentals=copies * ff),
        name=name,
    )(table, meta, x, dy, slot, slot_t, gate, wd, w1, w3, w2)


def solution(mesh):
    tok_spec = P(TOK_AXES, None)
    route_spec = P(None, TOK_AXES, None)
    expert_spec = P(None, "ep", None, None)
    whole_spec = P(None, None, None)
    reps, eps, dps = (mesh.shape[a] for a in TOK_AXES)

    def device_step(tok_in, tok_grad, route_ids, gate_vals, w_dense, w_gate, w_up, w_down):
        layers, held = w_gate.shape[:2]
        experts = held * eps
        share = held // (reps * dps)
        x_id, rest = route_ids // held, route_ids % held
        r_id, rest = rest // (dps * share), rest % (dps * share)
        ids = (r_id * eps + x_id) * (dps * share) + rest
        mine = (lax.axis_index("rep") * dps + lax.axis_index("dp")) * share

        def gather(w, l):
            return lax.all_gather(lax.dynamic_slice_in_dim(w[l], mine, share, 0), TOK_AXES, axis=0, tiled=True)

        weights = [tuple(gather(w, l) for w in (w_gate, w_up, w_down)) for l in range(layers)]
        slot, table, meta = route_tables(ids.transpose(0, 2, 1), experts)
        slot_t = slot.transpose(0, 2, 1)

        def layer(l, fwd, bwd, x, dy, name):
            return run_layer(fwd, bwd, x, dy, slot[l], slot_t[l], gate_vals[l], table[l], meta[l], w_dense[l], *weights[l], name)

        def reduce_weight(g):
            part = lax.psum_scatter(g, TOK_AXES, scatter_dimension=0, tiled=True)
            return lax.all_gather(part, ("rep", "dp"), axis=0, tiled=True)

        current = [tok_in]
        for l in range(layers - 1):
            current.append(layer(l, True, False, current[-1], current[-1], f"fwd_{l}")[0])
        grad = tok_grad
        sums = [None] * layers
        for l in reversed(range(layers)):
            last = l == layers - 1
            out = layer(l, last, True, current[l], grad, f"bwd_{l}")
            if last:
                tok_out, out = out[0], out[1:]
            grad = out[0]
            sums[l] = (out[1],) + tuple(reduce_weight(g) for g in out[2:])
        dense = lax.psum(jnp.stack([s[0] for s in sums]), TOK_AXES)
        return (tok_out, grad, dense) + tuple(jnp.stack([s[i] for s in sums]) for i in (1, 2, 3))

    return jax.shard_map(device_step, mesh=mesh, in_specs=(tok_spec, tok_spec, route_spec, route_spec, whole_spec, expert_spec, expert_spec, expert_spec), out_specs=(tok_spec, tok_spec, whole_spec, expert_spec, expert_spec, expert_spec), check_vma=False)
```

time: 1930 us -> 838 us (0.43)
  local copies, waits for them, and re-layouts: 825 us -> 36.1 us
  matrix products: 452 us -> 0.19 us
  Pallas kernels: 0 us -> 260 us
  other arithmetic: 178 us -> 15.4 us
  waiting for transfers between devices: 395 us -> 511 us
  starting transfers between devices: 56.8 us -> 0.75 us
    gather x10 -> x0, local copies, waits for them, and re-layouts: 583 us -> none  [the longest x2 181 us: layer_backward(): slot_gate = jnp.take(gate_pad, copy_of)]
    dot_general x24 -> x1, matrix products: 452 us -> 0.19 us  [dot_nn(): return jnp.dot(a, b, preferred_element_type=F32)]
    all_to_all x8 -> x0, waiting for transfers between devices: 346 us -> none  [the longest x2 148 us: layer_forward(): lax.all_to_all(expert_out, 'ep', 1, 0, tiled=True)]
    pallas_call x0 -> x3, Pallas kernels: none -> 260 us  [run_layer(): pl.pallas_call(functools.partial(layer_kernel, cfg), out_shape=out_shape,...]
    reduce_scatter x0 -> x6, waiting for transfers between devices: none -> 256 us  [reduce_weight(): part = lax.psum_scatter(g, TOK_AXES, scatter_dimension=0, tiled=True)]
    all_gather x0 -> x12, waiting for transfers between devices: none -> 210 us  [the longest x6 108 us: reduce_weight(): return lax.all_gather(part, ('rep', 'dp'), axis=0, tiled=True)]
    reduce_sum x6 -> x7, other arithmetic: 98.1 us -> 1.26 us  [the longest x1 0.35 us: route_tables(): jnp.sum(grans[:, :, None, :] * lower_k[None, None], axis=3)]
    convert_element_type x8 -> x0, local copies, waits for them, and re-layouts: 91.7 us -> none  [the longest x2 24.5 us: layer_backward(): (jnp.einsum('enf,edf->end', grad_gate_act, gate_w, preferred_element_type...]
  transfers between devices with their start and end apart: 11 -> 19, of which waited for: 8 -> 17; matrix products, arithmetic and copies ran while one was open for 40% -> 5% of each run, Pallas kernels for 0% -> 6%
where the time goes in v1:
time: 838 us
  waiting for transfers between devices  511 us (61%)
  Pallas kernels  260 us (31%)
  local copies, waits for them, and re-layouts  36.1 us (4%)
  other arithmetic  15.4 us (2%)
  between operations  14.2 us (2%)
    pallas_call x3, Pallas kernels, run_layer(): pl.pallas_call(functools.partial(layer_kernel, cfg), out_shape=out_shape,...  260 us
    reduce_scatter x6, waiting for transfers between devices, reduce_weight(): part = lax.psum_scatter(g, TOK_AXES, scatter_dimension=0, tiled=True)  256 us
    all_gather x6, waiting for transfers between devices, reduce_weight(): return lax.all_gather(part, ('rep', 'dp'), axis=0, tiled=True)  108 us
    all_gather x6, waiting for transfers between devices, gather(): lax.all_gather(lax.dynamic_slice_in_dim(w[l], mine, share, 0), TOK_AXES,...  102 us
    psum x1, waiting for transfers between devices, device_step(): dense = lax.psum(jnp.stack([s[0] for s in sums]), TOK_AXES)  42 us
  transfers between devices with their start and end apart: 19, of which 17 were waited for; matrix products, arithmetic and copies ran while one was open for 5% of the time, Pallas kernels for 6%

profile of v1, /device:TPU:0, one launch (start us, length us, event | category | flops | bytes accessed | tf_op | source)
XLA Modules:
  0.0 837.6 jit_solution(17216722173963684324)
XLA Ops:
  7.2 3.6 fusion.14
  10.8 1.8 constant_dynamic-slice_fusion.5
  12.7 3.6 fusion.13
  16.3 0.8 constant_dynamic-slice_fusion.4
  17.2 3.5 fusion.12
  20.7 0.8 constant_dynamic-slice_fusion.3
  21.6 0.8 constant_dynamic-slice_fusion.2
  22.5 1.9 constant_dynamic-slice_fusion.1
  24.5 1.8 constant_dynamic-slice_fusion
  26.4 0.5 fusion.6
  26.9 0.1 reduce_or.12
  27.0 0.1 convert_reduce_fusion
  27.1 0.1 sub.63
  27.2 0.2 fusion.11
  27.4 0.2 multiply_reduce_fusion.2
  27.6 0.6 squeeze.51.meta
  28.1 0.7 squeeze.49.meta
  28.8 0.1 multiply_reduce_fusion.1
  29.0 0.3 multiply_reduce_fusion
  29.4 0.1 add_bitcast_fusion
  29.4 0.1 copy.47
  29.6 0.1 copy.46
  29.7 0.2 select_reduce_fusion.1
  29.9 0.7 squeeze.50.table
  30.5 0.7 squeeze.48.table
  31.2 0.2 convolution_convert_fusion
  31.5 2.0 copy.53
  33.5 2.0 copy.52
  35.5 0.1 add.157
  35.6 0.2 select_reduce_fusion
  35.8 2.6 copy.49
  38.5 0.7 slice_bitcast_fusion.2
  39.2 0.6 slice_bitcast_fusion.4
  39.8 4.6 slice_bitcast_fusion
  44.4 30.8 %all-gather.33.cloned.1.call-done = bf16[8,1,256,896]{3,2,1,0:T(8,128)(2,1)} async-done(((bf16[1,1,256,896]{3,2,1,0:T(8,128)(2,1)}), bf16[8,1,256,896]{3,2,1,0:T(8,128)(2,1)}) %all-gather.33.cloned.1.call-update) | async-done | bytes 3670032 | tf_op jit(solution)/shard_map/all_gather | solution.py:259
  75.3 31.0 %all-gather.35.cloned.1.call-done = bf16[8,1,896,256]{3,2,1,0:T(8,128)(2,1)} async-done(((bf16[1,1,896,256]{3,2,1,0:T(8,128)(2,1)}), bf16[8,1,896,256]{3,2,1,0:T(8,128)(2,1)}) %all-gather.35.cloned.1.call-update) | async-done | bytes 3670032 | tf_op jit(solution)/shard_map/all_gather | solution.py:259
  106.2 50.7 %fwd_0.1.x_ref = bf16[4096,256]{1,0:T(8,128)(2,1)} custom-call(s32[640]{0:T(1024)} %squeeze.50.table, s32[24]{0:T(128)} %squeeze.51.meta, bf16[4096,256]{1,0:T(8,128)(2,1)} %x_ref.3, bf16[4096,256]{1,0:T(8,128)(2,1)} %x_ref.3, s32[2,4096]{1,0:T(2,128)} %get-tuple-element.45.slot_r, s32[4096,2]{1,0:T(8,128)} %get-tuple-element.33.slot_c, f32[4096,2]{1,0:T(8,128)} %bitcast.45, ...), custom_call_target="tpu_custom_call" | custom-call | flops 11274289152 | bytes 11010048 | tf_op jit(solution)/shard_map/fwd_0/pallas_call | solution.py:232
  156.9 9.9 %all-gather.39.cloned.1.call-done = bf16[8,1,256,896]{3,2,1,0:T(8,128)(2,1)} async-done(((bf16[1,1,256,896]{3,2,1,0:T(8,128)(2,1)}), bf16[8,1,256,896]{3,2,1,0:T(8,128)(2,1)}) %all-gather.39.cloned.1.call-update) | async-done | bytes 3670032 | tf_op jit(solution)/shard_map/all_gather | solution.py:259
  166.8 30.2 %all-gather.41.cloned.1.call-done = bf16[8,1,896,256]{3,2,1,0:T(8,128)(2,1)} async-done(((bf16[1,1,896,256]{3,2,1,0:T(8,128)(2,1)}), bf16[8,1,896,256]{3,2,1,0:T(8,128)(2,1)}) %all-gather.41.cloned.1.call-update) | async-done | bytes 3670032 | tf_op jit(solution)/shard_map/all_gather | solution.py:259
  197.0 107.4 %bwd_1.1 = (bf16[4096,256]{1,0:T(8,128)(2,1)}, bf16[4096,256]{1,0:T(8,128)(2,1)}, bf16[256,256]{1,0:T(8,128)(2,1)}, bf16[8,256,896]{2,1,0:T(8,128)(2,1)}, bf16[8...) custom-call(s32[640]{0:T(1024)} %squeeze.48.table, s32[24]{0:T(128)} %squeeze.49.meta, ...), custom_call_target="tpu_custom_call" | custom-call | flops 33822867456 | bytes 11010048 | tf_op jit(solution)/shard_map/bwd_1/pallas_call | solution.py:232
  304.4 101.8 %bwd_0.1 = (bf16[4096,256]{1,0:T(8,128)(2,1)}, bf16[256,256]{1,0:T(8,128)(2,1)}, bf16[8,256,896]{2,1,0:T(8,128)(2,1)}, bf16[8,256,896]{2,1,0:T(8,128)(2,1)}, bf16[8,896,256]{2,1,0:T(8,128)(2,1)}) custom-call(s32[640]{0:T(1024)} %squeeze.50.table, s32[24]{0:T(128)} %squeeze.51.meta, bf16[4096,256]{1,0:T(8,128)(2,1)} %x_ref.3, ...), custom_call_target="tpu_custom_call" | custom-call | flops 30064771072 | bytes 11010048 | tf_op jit(solution)/shard_map/bwd_0/pallas_call | solution.py:232
  406.3 0.7 reduce-scatter.9.cloned.1.call-update
  407.0 0.7 reduce-scatter.11.cloned.1.call-update
  407.7 0.5 reduce-scatter.13.cloned.1.call-update
  408.3 0.7 reduce-scatter.15.cloned.1.call-update
  409.1 0.5 reduce-scatter.17.cloned.1.call-update
  409.7 38.3 %reduce-scatter.7.cloned.1.call-done = bf16[1,256,896]{2,1,0:T(8,128)(2,1)} async-done(((bf16[8,256,896]{2,1,0:T(8,128)(2,1)}), bf16[1,256,896]{2,1,0:T(8,128)(2,1)}) %reduce-scatter.7.cloned.1.call-update) | async-done | bytes 458768 | tf_op jit(solution)/shard_map/reduce_scatter | solution.py:269
  448.1 43.8 %reduce-scatter.9.cloned.1.call-done = bf16[1,256,896]{2,1,0:T(8,128)(2,1)} async-done(((bf16[8,256,896]{2,1,0:T(8,128)(2,1)}), bf16[1,256,896]{2,1,0:T(8,128)(2,1)}) %reduce-scatter.9.cloned.1.call-update) | async-done | bytes 458768 | tf_op jit(solution)/shard_map/reduce_scatter | solution.py:269
  492.0 43.3 %reduce-scatter.11.cloned.1.call-done = bf16[1,256,896]{2,1,0:T(8,128)(2,1)} async-done(((bf16[8,256,896]{2,1,0:T(8,128)(2,1)}), bf16[1,256,896]{2,1,0:T(8,128)(2,1)}) %reduce-scatter.11.cloned.1.call-update) | async-done | bytes 458768 | tf_op jit(solution)/shard_map/reduce_scatter | solution.py:269
  535.3 43.7 %reduce-scatter.13.cloned.1.call-done = bf16[1,256,896]{2,1,0:T(8,128)(2,1)} async-done(((bf16[8,256,896]{2,1,0:T(8,128)(2,1)}), bf16[1,256,896]{2,1,0:T(8,128)(2,1)}) %reduce-scatter.13.cloned.1.call-update) | async-done | bytes 458768 | tf_op jit(solution)/shard_map/reduce_scatter | solution.py:269
  579.0 43.3 %reduce-scatter.15.cloned.1.call-done = bf16[1,896,256]{2,1,0:T(8,128)(2,1)} async-done(((bf16[8,896,256]{2,1,0:T(8,128)(2,1)}), bf16[1,896,256]{2,1,0:T(8,128)(2,1)}) %reduce-scatter.15.cloned.1.call-update) | async-done | bytes 458768 | tf_op jit(solution)/shard_map/reduce_scatter | solution.py:269
  622.4 43.7 %reduce-scatter.17.cloned.1.call-done = bf16[1,896,256]{2,1,0:T(8,128)(2,1)} async-done(((bf16[8,896,256]{2,1,0:T(8,128)(2,1)}), bf16[1,896,256]{2,1,0:T(8,128)(2,1)}) %reduce-scatter.17.cloned.1.call-update) | async-done | bytes 458768 | tf_op jit(solution)/shard_map/reduce_scatter | solution.py:269
  666.2 0.7 pad_maximum_fusion.3
  666.9 18.8 %all-gather.19.cloned.1.call-done = bf16[4,256,896]{2,1,0:T(8,128)(2,1)} async-done(((bf16[1,256,896]{2,1,0:T(8,128)(2,1)}), bf16[4,256,896]{2,1,0:T(8,128)(2,1)}) %all-gather.19.cloned.1.call-update) | async-done | bytes 1835024 | tf_op jit(solution)/shard_map/all_gather | solution.py:270
  685.7 19.5 %all-gather.21.cloned.1.call-done = bf16[4,256,896]{2,1,0:T(8,128)(2,1)} async-done(((bf16[1,256,896]{2,1,0:T(8,128)(2,1)}), bf16[4,256,896]{2,1,0:T(8,128)(2,1)}) %all-gather.21.cloned.1.call-update) | async-done | bytes 1835024 | tf_op jit(solution)/shard_map/all_gather | solution.py:270
  705.2 4.3 pad_maximum_fusion
  709.5 15.2 %all-gather.23.cloned.1.call-done = bf16[4,256,896]{2,1,0:T(8,128)(2,1)} async-done(((bf16[1,256,896]{2,1,0:T(8,128)(2,1)}), bf16[4,256,896]{2,1,0:T(8,128)(2,1)}) %all-gather.23.cloned.1.call-update) | async-done | bytes 1835024 | tf_op jit(solution)/shard_map/all_gather | solution.py:270
  724.7 19.5 %all-gather.25.cloned.1.call-done = bf16[4,256,896]{2,1,0:T(8,128)(2,1)} async-done(((bf16[1,256,896]{2,1,0:T(8,128)(2,1)}), bf16[4,256,896]{2,1,0:T(8,128)(2,1)}) %all-gather.25.cloned.1.call-update) | async-done | bytes 1835024 | tf_op jit(solution)/shard_map/all_gather | solution.py:270
  744.2 4.3 pad_maximum_fusion.1
  748.4 15.2 %all-gather.27.cloned.1.call-done = bf16[4,896,256]{2,1,0:T(8,128)(2,1)} async-done(((bf16[1,896,256]{2,1,0:T(8,128)(2,1)}), bf16[4,896,256]{2,1,0:T(8,128)(2,1)}) %all-gather.27.cloned.1.call-update) | async-done | bytes 1835024 | tf_op jit(solution)/shard_map/all_gather | solution.py:270
  763.7 19.5 %all-gather.29.cloned.1.call-done = bf16[4,896,256]{2,1,0:T(8,128)(2,1)} async-done(((bf16[1,896,256]{2,1,0:T(8,128)(2,1)}), bf16[4,896,256]{2,1,0:T(8,128)(2,1)}) %all-gather.29.cloned.1.call-update) | async-done | bytes 1835024 | tf_op jit(solution)/shard_map/all_gather | solution.py:270
  783.2 4.2 pad_maximum_fusion.2
  787.4 42.0 %all-reduce.2.cloned.1.call-done = bf16[2,256,256]{2,1,0:T(8,128)(2,1)} async-done(((bf16[2,256,256]{2,1,0:T(8,128)(2,1)}), bf16[2,256,256]{2,1,0:T(8,128)(2,1)}) %all-reduce.2.cloned.1.call-update) | async-done | bytes 262160 | tf_op jit(solution)/shard_map/psum | solution.py:284
  829.4 1.7 copy.56
  (62 shorter events, 1.4 us)
Async XLA Ops:
  7.2 37.3 %all-gather.31.cloned.1.call-start = ((), (), s32[]{:S(2)}) async-start(), calls=%async_computation.19 | async-start | bytes 4128768 | tf_op jit(solution)/shard_map/all_gather | solution.py:259
  12.7 62.6 %all-gather.33.cloned.1.call-start = ((), (), s32[]{:S(2)}) async-start(), calls=%async_computation.20 | async-start | bytes 4128768 | tf_op jit(solution)/shard_map/all_gather | solution.py:259
  17.1 89.1 %all-gather.35.cloned.1.call-start = ((), (), s32[]{:S(2)}) async-start(), calls=%async_computation.21 | async-start | bytes 4128768 | tf_op jit(solution)/shard_map/all_gather | solution.py:259
  21.5 4.8 copy-start.3
  21.6 135.4 %all-gather.37.cloned.1.call-start = ((), (), s32[]{:S(2)}) async-start(), calls=%async_computation.22 | async-start | bytes 4128768 | tf_op jit(solution)/shard_map/all_gather | solution.py:259
  22.5 144.3 %all-gather.39.cloned.1.call-start = ((), (), s32[]{:S(2)}) async-start(), calls=%async_computation.23 | async-start | bytes 4128768 | tf_op jit(solution)/shard_map/all_gather | solution.py:259
  22.5 9.0 %copy-start.4 = (f32[2,4096,2]{1,2,0:T(2,128)S(1)}, f32[2,4096,2]{1,2,0:T(2,128)}, u32[]{:S(2)}) copy-start(f32[2,4096,2]{1,2,0:T(2,128)} %param.11) | copy-start | bytes 196612
  24.4 172.6 %all-gather.41.cloned.1.call-start = ((), (), s32[]{:S(2)}) async-start(), calls=%async_computation.24 | async-start | bytes 4128768 | tf_op jit(solution)/shard_map/all_gather | solution.py:259
  26.3 421.7 %reduce-scatter.7.cloned.1.call-start = ((), (), s32[]{:S(2)}) async-start(), calls=%async_computation.7 | async-start | bytes 4128768 | tf_op jit(solution)/shard_map/reduce_scatter | solution.py:269
  35.8 2.6 copy-start
  406.2 85.7 %reduce-scatter.9.cloned.1.call-start = ((), (), s32[]{:S(2)}) async-start(), calls=%async_computation.9 | async-start | bytes 4128768 | tf_op jit(solution)/shard_map/reduce_scatter | solution.py:269
  407.0 128.3 %reduce-scatter.11.cloned.1.call-start = ((), (), s32[]{:S(2)}) async-start(), calls=%async_computation.11 | async-start | bytes 4128768 | tf_op jit(solution)/shard_map/reduce_scatter | solution.py:269
  407.7 171.3 %reduce-scatter.13.cloned.1.call-start = ((), (), s32[]{:S(2)}) async-start(), calls=%async_computation.13 | async-start | bytes 4128768 | tf_op jit(solution)/shard_map/reduce_scatter | solution.py:269
  408.3 214.0 %reduce-scatter.15.cloned.1.call-start = ((), (), s32[]{:S(2)}) async-start(), calls=%async_computation.15 | async-start | bytes 4128768 | tf_op jit(solution)/shard_map/reduce_scatter | solution.py:269
  409.0 257.0 %reduce-scatter.17.cloned.1.call-start = ((), (), s32[]{:S(2)}) async-start(), calls=%async_computation.17 | async-start | bytes 4128768 | tf_op jit(solution)/shard_map/reduce_scatter | solution.py:269
  409.6 256.5 %copy-start.1 = (bf16[256,256]{1,0:T(8,128)(2,1)S(1)}, bf16[256,256]{1,0:T(8,128)(2,1)}, u32[]{:S(2)}) copy-start(bf16[256,256]{1,0:T(8,128)(2,1)} %get-tuple-element.21) | copy-start | bytes 393220
  409.6 256.5 %copy-start.2 = (bf16[256,256]{1,0:T(8,128)(2,1)S(1)}, bf16[256,256]{1,0:T(8,128)(2,1)}, u32[]{:S(2)}) copy-start(bf16[256,256]{1,0:T(8,128)(2,1)} %get-tuple-element.20) | copy-start | bytes 393220
  409.6 276.1 %all-gather.19.cloned.1.call-start = ((), (), s32[]{:S(2)}) async-start(), calls=%async_computation.8 | async-start | bytes 2293760 | tf_op jit(solution)/shard_map/all_gather | solution.py:270
  448.0 257.2 %all-gather.21.cloned.1.call-start = ((), (), s32[]{:S(2)}) async-start(), calls=%async_computation.10 | async-start | bytes 2293760 | tf_op jit(solution)/shard_map/all_gather | solution.py:270
  491.9 232.8 %all-gather.23.cloned.1.call-start = ((), (), s32[]{:S(2)}) async-start(), calls=%async_computation.12 | async-start | bytes 2293760 | tf_op jit(solution)/shard_map/all_gather | solution.py:270
  535.3 208.9 %all-gather.25.cloned.1.call-start = ((), (), s32[]{:S(2)}) async-start(), calls=%async_computation.14 | async-start | bytes 2293760 | tf_op jit(solution)/shard_map/all_gather | solution.py:270
  579.0 184.7 %all-gather.27.cloned.1.call-start = ((), (), s32[]{:S(2)}) async-start(), calls=%async_computation.16 | async-start | bytes 2293760 | tf_op jit(solution)/shard_map/all_gather | solution.py:270
  622.3 160.8 %all-gather.29.cloned.1.call-start = ((), (), s32[]{:S(2)}) async-start(), calls=%async_computation.18 | async-start | bytes 2293760 | tf_op jit(solution)/shard_map/all_gather | solution.py:270
  666.1 163.3 %all-reduce.2.cloned.1.call-start = ((), (), s32[]{:S(2)}) async-start(), calls=%async_computation.6 | async-start | bytes 524288 | tf_op jit(solution)/shard_map/psum | solution.py:284
Sparse Core Ops, SparseCore 0:
  12.8 31.4 all-gather.30
  46.7 28.5 all-gather.32
  77.6 28.5 all-gather.34
  107.9 28.6 all-gather.36
  138.2 28.5 all-gather.38
  168.4 28.5 all-gather.40
  406.3 41.6 reduce-scatter.6
  451.9 39.9 reduce-scatter.8
  495.3 39.9 reduce-scatter.10
  539.0 39.9 reduce-scatter.12
  582.4 39.9 reduce-scatter.14
  626.1 39.9 reduce-scatter.16
  667.6 18.0 all-gather.18
  687.1 18.0 all-gather.20
  706.6 18.0 all-gather.22
  726.1 18.0 all-gather.24
  745.6 18.0 all-gather.26
  765.1 18.0 all-gather.28
  786.8 42.5 all-reduce.1

commit v2 on v1

--- a/solution.py
+++ b/solution.py
@@ -239,6 +239,165 @@
     )(table, meta, x, dy, slot, slot_t, gate, wd, w1, w3, w2)
 
 
+def swap(src, dst, send, recv, i, where):
+    return pltpu.make_async_remote_copy(src_ref=src, dst_ref=dst, send_sem=send.at[i], recv_sem=recv.at[i], device_id=where, device_id_type=pl.DeviceIdType.MESH)
+
+
+def add_into(dst, a, b):
+    dst[...] = (a[...].astype(F32) + b[...].astype(F32)).astype(BF16)
+
+
+def reduce_kernel(n, parts, *refs):
+    grads, refs = refs[:n], refs[n:]
+    dense, refs = refs[0], refs[1:]
+    outs, refs = refs[:n], refs[n:]
+    dense_out, refs = refs[0], refs[1:]
+    r1, refs = refs[:n], refs[n:]
+    a1, refs = refs[:n], refs[n:]
+    r2, refs = refs[:n], refs[n:]
+    r3, refs = refs[:n], refs[n:]
+    dr, da, send, recv = refs
+    r, x, d = (lax.axis_index(a) for a in TOK_AXES)
+    over_r, over_x, over_d = (1 - r, x, d), (r, 1 - x, d), (r, x, 1 - d)
+    barrier = pltpu.get_barrier_semaphore()
+    for where in (over_r, over_x, over_d):
+        pl.semaphore_signal(barrier, inc=1, device_id=where, device_id_type=pl.DeviceIdType.MESH)
+    pl.semaphore_wait(barrier, 3)
+
+    pieces = []
+    for i in range(n):
+        rows = grads[i].shape[1] // parts
+        pieces += [(i, slice(p * rows, (p + 1) * rows)) for p in range(parts)]
+    count = len(pieces)
+    per = 10
+
+    def cp(c, k, src, dst, where):
+        return swap(src, dst, send, recv, c * per + k, where)
+
+    def slab(rr, xx, dd):
+        return rr * 4 + xx * 2 + dd
+
+    def s1(c):
+        i, rows = pieces[c]
+        out = []
+        for q in range(4):
+            xx = 1 - x if q < 2 else x
+            rr = q % 2
+            out.append(cp(c, q, grads[i].at[slab(rr, xx, 1 - d), rows], r1[i].at[q, rows], over_d))
+        return out
+
+    def s2(c):
+        i, rows = pieces[c]
+        return [cp(c, 4 + q, a1[i].at[q, rows], r2[i].at[q, rows], over_x) for q in range(2)]
+
+    def s3(c):
+        i, rows = pieces[c]
+        return cp(c, 6, a1[i].at[3 - r, rows], r3[i].at[rows], over_r)
+
+    def s4(c):
+        i, rows = pieces[c]
+        own = r * 2 + d
+        mine = outs[i].at[own, rows]
+        return cp(c, 7, mine, mine, over_r), cp(c, 8, mine, mine, over_d)
+
+    def s5(c):
+        i, rows = pieces[c]
+        other = outs[i].at[(1 - r) * 2 + d, rows]
+        return cp(c, 9, other, other, over_d)
+
+    base = count * per
+
+    def dense_copy(k, where):
+        return swap(dense if k == 0 else da.at[k - 1], dr.at[k], send, recv, base + k, where)
+
+    dense_copy(0, over_d).start()
+    for c in range(count):
+        for q in s1(c):
+            q.start()
+
+    def step2(c):
+        i, rows = pieces[c]
+        copies = s1(c)
+        for q in range(4):
+            xx = 1 - x if q < 2 else x
+            copies[q].wait_recv()
+            add_into(a1[i].at[q, rows], grads[i].at[slab(q % 2, xx, d), rows], r1[i].at[q, rows])
+            if q == 1:
+                for t in s2(c):
+                    t.start()
+
+    def step3(c):
+        i, rows = pieces[c]
+        for t in s2(c):
+            t.wait_recv()
+        add_into(a1[i].at[3 - r, rows], a1[i].at[3 - r, rows], r2[i].at[1 - r, rows])
+        s3(c).start()
+        add_into(a1[i].at[2 + r, rows], a1[i].at[2 + r, rows], r2[i].at[r, rows])
+
+    def step4(c):
+        i, rows = pieces[c]
+        s3(c).wait_recv()
+        add_into(outs[i].at[r * 2 + d, rows], a1[i].at[2 + r, rows], r3[i].at[rows])
+        for t in s4(c):
+            t.start()
+
+    def step5(c):
+        back, _ = s4(c)
+        back.wait_recv()
+        s5(c).start()
+
+    def dense_step(k):
+        last = da.at[k - 2] if k > 1 else dense
+        where = (over_d, over_x, over_r)
+        dense_copy(k - 1, where[k - 1]).wait_recv()
+        if k < 3:
+            add_into(da.at[k - 1], last, dr.at[k - 1])
+            dense_copy(k, where[k]).start()
+        else:
+            add_into(dense_out, last, dr.at[k - 1])
+
+    for t in range(count + 4):
+        if t < count:
+            step2(t)
+        if 1 <= t <= 3:
+            dense_step(t)
+        if 0 <= t - 2 < count:
+            step3(t - 2)
+        if 0 <= t - 3 < count:
+            step4(t - 3)
+        if 0 <= t - 4 < count:
+            step5(t - 4)
+    for c in range(count):
+        for t in s1(c) + s2(c) + [s3(c)]:
+            t.wait_send()
+        back, beside = s4(c)
+        back.wait_send()
+        beside.wait()
+        s5(c).wait()
+    for k, where in enumerate((over_d, over_x, over_r)):
+        dense_copy(k, where).wait_send()
+
+
+def reduce_grads(grads, dense, parts, cid, name):
+    n = len(grads)
+    vmem = pl.BlockSpec(memory_space=pltpu.VMEM)
+    shapes = [g.shape[1:] for g in grads]
+
+    def bufs(lead):
+        return [pltpu.VMEM(lead + s, BF16) for s in shapes]
+
+    sems = n * parts * 10 + 3
+    return pl.pallas_call(
+        functools.partial(reduce_kernel, n, parts),
+        out_shape=[jax.ShapeDtypeStruct((4,) + s, BF16) for s in shapes] + [jax.ShapeDtypeStruct(dense.shape, BF16)],
+        in_specs=[vmem] * (n + 1),
+        out_specs=[vmem] * (n + 1),
+        scratch_shapes=bufs((4,)) + bufs((4,)) + bufs((2,)) + bufs(()) + [pltpu.VMEM((3,) + dense.shape, BF16), pltpu.VMEM((2,) + dense.shape, BF16), pltpu.SemaphoreType.DMA((sems,)), pltpu.SemaphoreType.DMA((sems,))],
+        compiler_params=pltpu.CompilerParams(collective_id=cid, has_side_effects=True, vmem_limit_bytes=60 * 1024 * 1024),
+        name=name,
+    )(*grads, dense)
+
+
 def solution(mesh):
     tok_spec = P(TOK_AXES, None)
     route_spec = P(None, TOK_AXES, None)
@@ -265,9 +424,11 @@
         def layer(l, fwd, bwd, x, dy, name):
             return run_layer(fwd, bwd, x, dy, slot[l], slot_t[l], gate_vals[l], table[l], meta[l], w_dense[l], *weights[l], name)
 
-        def reduce_weight(g):
-            part = lax.psum_scatter(g, TOK_AXES, scatter_dimension=0, tiled=True)
-            return lax.all_gather(part, ("rep", "dp"), axis=0, tiled=True)
+        def scatter_sum(g):
+            return lax.psum_scatter(g, TOK_AXES, scatter_dimension=0, tiled=True)
+
+        def gather_back(g):
+            return lax.all_gather(g, ("rep", "dp"), axis=0, tiled=True)
 
         current = [tok_in]
         for l in range(layers - 1):
@@ -280,8 +441,15 @@
             if last:
                 tok_out, out = out[0], out[1:]
             grad = out[0]
-            sums[l] = (out[1],) + tuple(reduce_weight(g) for g in out[2:])
-        dense = lax.psum(jnp.stack([s[0] for s in sums]), TOK_AXES)
+            for m in range(l + 1, layers):
+                *parts, grad = lax.optimization_barrier((*sums[m][1:], grad))
+                sums[m] = (sums[m][0],) + tuple(gather_back(g) for g in parts)
+            if l > 0:
+                sums[l] = (out[1],) + tuple(scatter_sum(g) for g in out[2:])
+            else:
+                dense = jnp.stack([out[1]] + [s[0] for s in sums[1:]])
+                *reduced, dense = reduce_grads(out[2:], dense, 2, 0, "reduce_0")
+                sums[0] = (None,) + tuple(reduced)
         return (tok_out, grad, dense) + tuple(jnp.stack([s[i] for s in sums]) for i in (1, 2, 3))
 
     return jax.shard_map(device_step, mesh=mesh, in_specs=(tok_spec, tok_spec, route_spec, route_spec, whole_spec, expert_spec, expert_spec, expert_spec), out_specs=(tok_spec, tok_spec, whole_spec, expert_spec, expert_spec, expert_spec), check_vma=False)

time: 838 us -> 571 us (0.68)
  waiting for transfers between devices: 511 us -> 126 us
  Pallas kernels: 260 us -> 378 us
    reduce_scatter x6 -> x3, waiting for transfers between devices: 256 us -> 22.3 us  [scatter_sum(): return lax.psum_scatter(g, TOK_AXES, scatter_dimension=0, tiled=True)]
    pallas_call x0 -> x1, Pallas kernels: none -> 115 us  [reduce_grads(): pl.pallas_call(functools.partial(reduce_kernel, n, parts), out_shape=[jax...]
    all_gather x6 -> x3, waiting for transfers between devices: 108 us -> 0.02 us  [gather_back(): return lax.all_gather(g, ('rep', 'dp'), axis=0, tiled=True)]
    psum x1 -> x0, waiting for transfers between devices: 42 us -> none  [device_step(): dense = lax.psum(jnp.stack([s[0] for s in sums]), TOK_AXES)]
  transfers between devices with their start and end apart: 19 -> 12, of which waited for: 17 -> 5; matrix products, arithmetic and copies ran while one was open for 5% -> 7% of each run, Pallas kernels for 6% -> 47%
where the time goes in v2:
time: 571 us
  Pallas kernels  378 us (66%)
  waiting for transfers between devices  126 us (22%)
  local copies, waits for them, and re-layouts  35.3 us (6%)
  other arithmetic  16 us (3%)
  between operations  14.4 us (3%)
    pallas_call x3, Pallas kernels, run_layer(): pl.pallas_call(functools.partial(layer_kernel, cfg), out_shape=out_shape,...  263 us
    pallas_call x1, Pallas kernels, reduce_grads(): pl.pallas_call(functools.partial(reduce_kernel, n, parts), out_shape=[jax...  115 us
    all_gather x6, waiting for transfers between devices, gather(): lax.all_gather(lax.dynamic_slice_in_dim(w[l], mine, share, 0), TOK_AXES,...  101 us
    reduce_scatter x3, waiting for transfers between devices, scatter_sum(): return lax.psum_scatter(g, TOK_AXES, scatter_dimension=0, tiled=True)  22.3 us
    another operation x3, other arithmetic, device_step(): jnp.stack([s[i] for s in sums])  12.4 us
  transfers between devices with their start and end apart: 12, of which 5 were waited for; matrix products, arithmetic and copies ran while one was open for 7% of the time, Pallas kernels for 47%

profile of v2, /device:TPU:0, one launch (start us, length us, event | category | flops | bytes accessed | tf_op | source)
XLA Modules:
  0.0 570.7 jit_solution(18319584339468027230)
XLA Ops:
  7.2 3.6 fusion.14
  10.8 1.8 constant_dynamic-slice_fusion.5
  12.7 0.0 all-gather.24.cloned.1.call-start
  12.7 3.6 fusion.13
  16.3 0.8 constant_dynamic-slice_fusion.4
  17.1 0.0 all-gather.26.cloned.1.call-start
  17.2 3.5 fusion.12
  20.7 0.8 constant_dynamic-slice_fusion.3
  21.6 0.0 all-gather.28.cloned.1.call-start
  21.6 0.8 constant_dynamic-slice_fusion.2
  22.5 0.0 all-gather.30.cloned.1.call-start
  22.5 1.8 constant_dynamic-slice_fusion.1
  24.4 0.0 all-gather.32.cloned.1.call-start
  24.4 1.8 constant_dynamic-slice_fusion
  26.3 0.0 reduce-scatter.4.cloned.1.call-start
  26.4 0.5 fusion.6
  26.9 0.1 reduce_or.12
  27.0 0.1 convert_reduce_fusion
  27.1 0.1 sub.63
  27.2 0.2 fusion.11
  27.4 0.2 multiply_reduce_fusion.2
  27.6 0.7 squeeze.51.meta
  28.3 0.7 squeeze.49.meta
  28.9 0.1 multiply_reduce_fusion.1
  29.0 0.1 copy.48
  29.1 0.4 multiply_reduce_fusion
  29.5 0.1 add_bitcast_fusion
  29.6 0.1 copy.47
  29.6 0.1 copy.45
  29.7 0.1 copy.46
  29.8 0.2 select_reduce_fusion.1
  30.0 0.7 squeeze.50.table
  30.7 0.7 squeeze.48.table
  31.3 0.2 convolution_convert_fusion
  31.5 0.1 reshape.210
  31.6 2.0 copy.53
  33.6 2.0 copy.52
  35.6 0.1 add.149
  35.7 0.2 select_reduce_fusion
  35.9 2.6 copy.49
  38.6 0.7 slice_bitcast_fusion.2
  39.3 0.6 slice_bitcast_fusion.4
  39.9 4.6 slice_bitcast_fusion
  44.6 30.7 %all-gather.24.cloned.1.call-done = bf16[8,1,256,896]{3,2,1,0:T(8,128)(2,1)} async-done(((bf16[1,1,256,896]{3,2,1,0:T(8,128)(2,1)}), bf16[8,1,256,896]{3,2,1,0:T(8,128)(2,1)}) %all-gather.24.cloned.1.call-update) | async-done | bytes 3670032 | tf_op jit(solution)/shard_map/all_gather | solution.py:418
  75.2 31.0 %all-gather.26.cloned.1.call-done = bf16[8,1,896,256]{3,2,1,0:T(8,128)(2,1)} async-done(((bf16[1,1,896,256]{3,2,1,0:T(8,128)(2,1)}), bf16[8,1,896,256]{3,2,1,0:T(8,128)(2,1)}) %all-gather.26.cloned.1.call-update) | async-done | bytes 3670032 | tf_op jit(solution)/shard_map/all_gather | solution.py:418
  106.2 51.5 %fwd_0.1.x_ref = bf16[4096,256]{1,0:T(8,128)(2,1)} custom-call(s32[640]{0:T(1024)} %squeeze.50.table, s32[24]{0:T(128)} %squeeze.51.meta, bf16[4096,256]{1,0:T(8,128)(2,1)} %x_ref.3, bf16[4096,256]{1,0:T(8,128)(2,1)} %x_ref.3, s32[2,4096]{1,0:T(2,128)} %get-tuple-element.61.slot_r, s32[4096,2]{1,0:T(8,128)} %get-tuple-element.49.slot_c, f32[4096,2]{1,0:T(8,128)} %bitcast.45, ...), custom_call_target="tpu_custom_call" | custom-call | flops 11274289152 | bytes 11010048 | tf_op jit(solution)/shard_map/fwd_0/pallas_call | solution.py:232
  157.7 9.0 %all-gather.30.cloned.1.call-done = bf16[8,1,256,896]{3,2,1,0:T(8,128)(2,1)} async-done(((bf16[1,1,256,896]{3,2,1,0:T(8,128)(2,1)}), bf16[8,1,256,896]{3,2,1,0:T(8,128)(2,1)}) %all-gather.30.cloned.1.call-update) | async-done | bytes 3670032 | tf_op jit(solution)/shard_map/all_gather | solution.py:418
  166.7 30.2 %all-gather.32.cloned.1.call-done = bf16[8,1,896,256]{3,2,1,0:T(8,128)(2,1)} async-done(((bf16[1,1,896,256]{3,2,1,0:T(8,128)(2,1)}), bf16[8,1,896,256]{3,2,1,0:T(8,128)(2,1)}) %all-gather.32.cloned.1.call-update) | async-done | bytes 3670032 | tf_op jit(solution)/shard_map/all_gather | solution.py:418
  197.0 107.4 %bwd_1.1 = (bf16[4096,256]{1,0:T(8,128)(2,1)}, bf16[4096,256]{1,0:T(8,128)(2,1)}, bf16[256,256]{1,0:T(8,128)(2,1)}, bf16[8,256,896]{2,1,0:T(8,128)(2,1)}, bf16[8...) custom-call(s32[640]{0:T(1024)} %squeeze.48.table, s32[24]{0:T(128)} %squeeze.49.meta, ...), custom_call_target="tpu_custom_call" | custom-call | flops 33822867456 | bytes 11010048 | tf_op jit(solution)/shard_map/bwd_1/pallas_call | solution.py:232
  304.4 0.0 reduce-scatter.6.cloned.1.call-start
  304.4 0.7 reduce-scatter.6.cloned.1.call-update
  305.2 0.7 reduce-scatter.8.cloned.1.call-update
  305.9 0.2 all-gather.16.cloned.1.call-start
  306.1 103.9 %bwd_0.1 = (bf16[4096,256]{1,0:T(8,128)(2,1)}, bf16[256,256]{1,0:T(8,128)(2,1)}, bf16[8,256,896]{2,1,0:T(8,128)(2,1)}, bf16[8,256,896]{2,1,0:T(8,128)(2,1)}, bf16[8,896,256]{2,1,0:T(8,128)(2,1)}) custom-call(s32[640]{0:T(1024)} %squeeze.50.table, s32[24]{0:T(128)} %squeeze.51.meta, bf16[4096,256]{1,0:T(8,128)(2,1)} %x_ref.3, ...), custom_call_target="tpu_custom_call" | custom-call | flops 30064771072 | bytes 11010048 | tf_op jit(solution)/shard_map/bwd_0/pallas_call | solution.py:232
  410.0 22.3 %reduce-scatter.8.cloned.1.call-done = bf16[1,896,256]{2,1,0:T(8,128)(2,1)} async-done(((bf16[8,896,256]{2,1,0:T(8,128)(2,1)}), bf16[1,896,256]{2,1,0:T(8,128)(2,1)}) %reduce-scatter.8.cloned.1.call-update) | async-done | bytes 458768 | tf_op jit(solution)/shard_map/reduce_scatter | solution.py:428
  432.4 0.7 all-gather.18.cloned.1.call-update
  433.1 0.0 all-gather.20.cloned.1.call-start
  433.1 0.5 all-gather.20.cloned.1.call-update
  433.7 1.6 pad_maximum_fusion.3.refs_3_
  435.3 115.4 %reduce_0.1 = (bf16[4,256,896]{2,1,0:T(8,128)(2,1)}, bf16[4,256,896]{2,1,0:T(8,128)(2,1)}, bf16[4,896,256]{2,1,0:T(8,128)(2,1)}, bf16[2,256,256]{2,1,0:T(8,128)(2,1)}) custom-call(bf16[8,256,896]{2,1,0:T(8,128)(2,1)} %get-tuple-element.32.refs_0_, bf16[8,256,896]{2,1,0:T(8,128)(2,1)} %get-tuple-element.33.refs_1_, ...), custom_call_target="tpu_custom_call" | custom-call | tf_op jit(solution)/shard_map/reduce_0/pallas_call | solution.py:390
  550.7 4.3 pad_maximum_fusion
  555.0 4.4 pad_maximum_fusion.1
  559.4 3.7 pad_maximum_fusion.2
  563.1 0.7 copy.56
  (44 shorter events, 0.5 us)
Async XLA Ops:
  7.2 37.4 %all-gather.22.cloned.1.call-start = ((), (), s32[]{:S(2)}) async-start(), calls=%async_computation.9 | async-start | bytes 4128768 | tf_op jit(solution)/shard_map/all_gather | solution.py:418
  12.7 62.5 %all-gather.24.cloned.1.call-start = ((), (), s32[]{:S(2)}) async-start(), calls=%async_computation.10 | async-start | bytes 4128768 | tf_op jit(solution)/shard_map/all_gather | solution.py:418
  17.1 89.0 %all-gather.26.cloned.1.call-start = ((), (), s32[]{:S(2)}) async-start(), calls=%async_computation.11 | async-start | bytes 4128768 | tf_op jit(solution)/shard_map/all_gather | solution.py:418
  21.5 4.8 copy-start.4
  21.6 136.2 %all-gather.28.cloned.1.call-start = ((), (), s32[]{:S(2)}) async-start(), calls=%async_computation.12 | async-start | bytes 4128768 | tf_op jit(solution)/shard_map/all_gather | solution.py:418
  22.5 144.3 %all-gather.30.cloned.1.call-start = ((), (), s32[]{:S(2)}) async-start(), calls=%async_computation.13 | async-start | bytes 4128768 | tf_op jit(solution)/shard_map/all_gather | solution.py:418
  22.5 9.1 %copy-start.5 = (f32[2,4096,2]{1,2,0:T(2,128)S(1)}, f32[2,4096,2]{1,2,0:T(2,128)}, u32[]{:S(2)}) copy-start(f32[2,4096,2]{1,2,0:T(2,128)} %param.11) | copy-start | bytes 196612
  24.4 172.6 %all-gather.32.cloned.1.call-start = ((), (), s32[]{:S(2)}) async-start(), calls=%async_computation.14 | async-start | bytes 4128768 | tf_op jit(solution)/shard_map/all_gather | solution.py:418
  26.3 383.7 %reduce-scatter.4.cloned.1.call-start = ((), (), s32[]{:S(2)}) async-start(), calls=%async_computation.3 | async-start | bytes 4128768 | tf_op jit(solution)/shard_map/reduce_scatter | solution.py:428
  35.9 2.7 copy-start.1
  304.4 105.6 %reduce-scatter.6.cloned.1.call-start = ((), (), s32[]{:S(2)}) async-start(), calls=%async_computation.4 | async-start | bytes 4128768 | tf_op jit(solution)/shard_map/reduce_scatter | solution.py:428
  305.1 127.2 %reduce-scatter.8.cloned.1.call-start = ((), (), s32[]{:S(2)}) async-start(), calls=%async_computation.5 | async-start | bytes 4128768 | tf_op jit(solution)/shard_map/reduce_scatter | solution.py:428
  305.9 244.9 %all-gather.16.cloned.1.call-start = ((), (), s32[]{:S(2)}) async-start(), calls=%async_computation.6 | async-start | bytes 2293760 | tf_op jit(solution)/shard_map/all_gather | solution.py:431
  306.1 127.6 %copy-start.3 = (bf16[256,256]{1,0:T(8,128)(2,1)S(1)}, bf16[256,256]{1,0:T(8,128)(2,1)}, u32[]{:S(2)}) copy-start(bf16[256,256]{1,0:T(8,128)(2,1)} %get-tuple-element.36) | copy-start | bytes 393220
  432.3 122.7 %all-gather.18.cloned.1.call-start = ((), (), s32[]{:S(2)}) async-start(), calls=%async_computation.7 | async-start | bytes 2293760 | tf_op jit(solution)/shard_map/all_gather | solution.py:431
  433.1 126.3 %all-gather.20.cloned.1.call-start = ((), (), s32[]{:S(2)}) async-start(), calls=%async_computation.8 | async-start | bytes 2293760 | tf_op jit(solution)/shard_map/all_gather | solution.py:431
  555.0 4.4 copy-start
  559.4 3.7 copy-start.2
Sparse Core Ops, SparseCore 0:
  12.8 31.3 all-gather.21
  46.6 28.5 all-gather.23
  77.6 28.5 all-gather.25
  107.8 28.6 all-gather.27
  138.2 28.5 all-gather.29
  168.4 28.5 all-gather.31
  304.5 39.9 reduce-scatter.3
  348.4 39.9 reduce-scatter.5
  392.4 39.8 reduce-scatter.7
  433.7 18.0 all-gather.15
  453.3 18.0 all-gather.17
  472.8 28.2 all-gather.19
